TPU v7x, 16 devices: a whole 2x2x2 slice. The times are simulated.
16 devices in a mesh: rep: 1, dp: 16 (over x, y, z, core).
Axes of the slice: x: 2, y: 2, z: 2, core: 2. Of those that a mesh axis runs over, the one named last changes fastest.
Arguments:
- x: bfloat16 [16, 2048, 1280], P(('rep', 'dp'))
- dy: bfloat16 [16, 2048, 1280], P(('rep', 'dp'))
- w_gate: bfloat16 [2, 1280, 4096], replicated
- w_up: bfloat16 [2, 1280, 4096], replicated
- w_down: bfloat16 [2, 4096, 1280], replicated
- m_w_gate: float32 [2, 1280, 4096], P(None, 'dp')
- m_w_up: float32 [2, 1280, 4096], P(None, 'dp')
- m_w_down: float32 [2, 4096, 1280], P(None, 'dp')
- v_w_gate: float32 [2, 1280, 4096], P(None, 'dp')
- v_w_up: float32 [2, 1280, 4096], P(None, 'dp')
- v_w_down: float32 [2, 4096, 1280], P(None, 'dp')
Outputs:
- output 1: bfloat16 [2, 1280, 4096], P('rep')
- output 2: bfloat16 [2, 1280, 4096], P('rep')
- output 3: bfloat16 [2, 4096, 1280], P('rep')
- output 4: float32 [2, 1280, 4096], P('rep', 'dp')
- output 5: float32 [2, 1280, 4096], P('rep', 'dp')
- output 6: float32 [2, 4096, 1280], P('rep', 'dp')
- output 7: float32 [2, 1280, 4096], P('rep', 'dp')
- output 8: float32 [2, 1280, 4096], P('rep', 'dp')
- output 9: float32 [2, 4096, 1280], P('rep', 'dp')
All inputs are finite; a program needn't handle non-finite values.
Results may differ from a plain program's by a relative error of at most 0.022.
Values are sent between devices in bfloat16 or wider.
A program may use at most 2 GiB of HBM per device.

v0:
```python
import jax
import jax.numpy as jnp
from jax import lax

NAMES = ("w_gate", "w_up", "w_down")


def matmul(a, w):
    return jnp.dot(a, w, preferred_element_type=jnp.float32).astype(jnp.bfloat16)


def normed(h):
    wide = h.astype(jnp.float32)
    scale = lax.rsqrt(jnp.mean(wide**2, -1, keepdims=True) + 1e-6)
    return (wide * scale).astype(jnp.bfloat16)


def layer(h, w):
    a = normed(h)
    gate = jnp.dot(a, w["w_gate"], preferred_element_type=jnp.float32)
    up = jnp.dot(a, w["w_up"], preferred_element_type=jnp.float32)
    return h + matmul((jax.nn.silu(gate) * up).astype(jnp.bfloat16), w["w_down"])


def adamw(w, m, v, g):
    m = 0.9 * m + 0.1 * g
    v = 0.95 * v + 0.05 * g * g
    step = m * lax.rsqrt(v + 1e-8) + 0.1 * w
    return (w - 0.02 * step).astype(jnp.bfloat16), m, v


def stack(weights, h):
    for number in range(weights["w_gate"].shape[0]):
        h = layer(h, {name: w[number] for name, w in weights.items()})
    return h


def solution(mesh):
    groups = mesh.shape["rep"]

    def step(x, dy, *arrays):
        weights, m, v = (arrays[i : i + 3] for i in (0, 3, 6))
        x, dy = (t.reshape(groups, -1, *t.shape[1:]) for t in (x, dy))

        def of_a_group(x, dy):
            _, back = jax.vjp(lambda w: stack(w, x), dict(zip(NAMES, weights, strict=True)))
            by_weights = back(dy)[0]
            gradients = [by_weights[name].astype(jnp.float32) for name in NAMES]
            new = [adamw(w.astype(jnp.float32), m, v, g) for w, m, v, g in zip(weights, m, v, gradients, strict=True)]
            return tuple(one[which] for which in range(3) for one in new)

        return tuple(t.reshape(-1, *t.shape[2:]) for t in jax.vmap(of_a_group)(x, dy))

    return step
```

profile of v0, /device:TPU:0, one launch (start us, length us, event | category | flops | bytes accessed | tf_op | source)
XLA Modules:
  0.0 2487.1 jit_solution(14971880630580223818)
XLA Ops:
  23.3 27.9 %fusion.173 = f32[2048,4096]{1,0:T(8,128)} fusion(bf16[2,1280,4096]{2,1,0:T(8,128)(2,1)} %param.12, bf16[1,2048,1280]{1,2,0:T(8,128)(2,1)S(1)} %fusion.157), kind=kOutput, calls=%fused_computation.224 | convolution fusion | flops 21474836480 | bytes 49283072 | tf_op jit(solution)/vmap(jvp())/dot_general | solution.py:20
  51.2 41.5 %fusion.150 = (bf16[1,2048,4096]{2,1,0:T(8,128)(2,1)}, f32[2048,4096]{1,0:T(8,128)}) fusion(f32[2048,4096]{1,0:T(8,128)} %fusion.173, bf16[2,1280,4096]{2,1,0:T(8,128)(2,1)} %param.17, bf16[1,2048,1280]{1,2,0:T(8,128)(2,1)} %copy-done), kind=kOutput, calls=%fused_computation.189 | convolution fusion | flops 21525168128 | bytes 99614720 | tf_op jit(solution)/vmap(jvp())/dot_general | solution.py:21
  92.7 30.4 %fusion.160 = (f32[2048]{0:T(1024)S(1)}, bf16[1,2048,1280]{1,2,0:T(8,128)(2,1)}) fusion(bf16[1,2048,1280]{1,2,0:T(8,128)(2,1)} %copy.1, bf16[2,4096,1280]{2,1,0:T(8,128)(2,1)} %param.15, bf16[1,2048,4096]{2,1,0:T(8,128)(2,1)} %get-tuple-element.263), kind=kOutput, calls=%fused_computation.211 | convolution fusion | flops 21487941632 | bytes 37756928 | tf_op jit(solution)/vmap(jvp())/dot_general | solution.py:9
  130.0 28.2 %fusion.166 = f32[2048,4096]{1,0:T(8,128)} fusion(bf16[2,1280,4096]{2,1,0:T(8,128)(2,1)} %param.17, bf16[1,2048,1280]{1,2,0:T(8,128)(2,1)S(1)} %fusion.161), kind=kOutput, calls=%fused_computation.217 | convolution fusion | flops 21474836480 | bytes 49283072 | tf_op jit(solution)/vmap(jvp())/dot_general | solution.py:21
  158.1 28.9 %convolution_convert_fusion.1 = bf16[2048,4096]{1,0:T(8,128)(2,1)} fusion(bf16[2,4096,1280]{2,1,0:T(8,128)(2,1)} %param.15, bf16[1,2048,1280]{2,1,0:T(8,128)(2,1)} %param.14), kind=kOutput, calls=%fused_computation.203 | convolution fusion | flops 21483225088 | bytes 32505856 | tf_op jit(solution)/vmap(transpose(jvp()))/dot_general | solution.py:9
  187.0 55.0 %fusion.139 = (bf16[1,2048,4096]{2,1,0:T(8,128)(2,1)}, bf16[1,2048,4096]{2,1,0:T(8,128)(2,1)}, f32[2048,4096]{1,0:T(8,128)}) fusion(f32[2048,4096]{1,0:T(8,128)} %fusion.166, bf16[2048,4096]{1,0:T(8,128)(2,1)} %convolution_convert_fusion.1, bf16[2,1280,4096]{2,1,0:T(8,128)(2,1)} %param.12, bf16[1,2048,1280]{1,2,0:T(8,128)(2,1)} %copy-done.1), kind=kOutput, calls=%fused_computation.173 | convolution fusion | flops 21600665600 | bytes 133169152 | tf_op jit(solution)/vmap(jvp())/dot_general | solution.py:20
  242.0 27.5 %fusion.149 = bf16[1,2048,4096]{2,1,0:T(8,128)(2,1)} fusion(f32[2048,4096]{1,0:T(8,128)} %fusion.166, f32[2048,4096]{1,0:T(8,128)} %get-tuple-element.267), kind=kLoop, calls=%fused_computation.187 | loop fusion | flops 50331648 | bytes 83886080 | tf_op jit(solution)/vmap(jvp())/convert_element_type | solution.py:22
  269.6 22.7 copy.3
  292.3 272.5 %while.16 = (bf16[1,2048,4096]{1,2,0:T(8,128)(2,1)}, bf16[1,2048,1280]{2,1,0:T(8,128)(2,1)}, f32[256,1280]{1,0:T(8,128)S(1)}, f32[256,1280]{1,0:T(8,128)}, u32[]...) while((bf16[1,2048,4096]{1,2,0:T(8,128)(2,1)}, ...), condition=%wide.windowed_dot_general_cond_rs.4.clone, body=%wide.windowed_dot_general_body_rs.4.clone.sunk | while | flops 5379063808 | bytes 91226696 | solution.py:9
  316.5 26.9 %collective-permute-start.18 = (f32[256,1280]{1,0:T(8,128)}, f32[256,1280]{1,0:T(8,128)S(1)}, u32[]{:S(2)}, u32[]{:S(2)}) collective-permute-start(f32[256,1280]{1,0:T(8,128)} %get-tuple-element.491), channel_id=31, source_target_pairs={{0,1},{1,2},{2,3},{3,4},{4,5},{5,6},{6,7},{7,8},{8,9},{9,10},{10,1... | collective-permute-start | bytes 3932168 | tf_op jit(solution)/vmap(transpose(jvp()))/dot_general | solution.py:9
  395.5 14.8 collective-permute-start.18
  429.5 14.9 collective-permute-start.16
  463.9 14.8 collective-permute-start.18
  497.9 14.8 collective-permute-start.16
  532.1 14.8 collective-permute-start.18
  564.8 14.8 collective-permute-start.28
  587.6 22.6 copy.5
  610.2 28.9 %fusion.190 = bf16[2048,1280]{0,1:T(8,128)(2,1)} fusion(bf16[2,1280,4096]{2,1,0:T(8,128)(2,1)} %param.17, bf16[1,2048,4096]{2,1,0:T(8,128)(2,1)} %get-tuple-element.612), kind=kOutput, calls=%fused_computation.237 | convolution fusion | flops 21474836480 | bytes 32505856 | tf_op jit(solution)/vmap(transpose(jvp()))/dot_general | solution.py:21
  639.1 31.4 %fusion.162 = (f32[2048]{0:T(1024)S(1)}, bf16[1,2048,1280]{1,2,0:T(8,128)(2,1)}) fusion(bf16[1,2048,1280]{1,2,0:T(8,128)(2,1)} %get-tuple-element.266, bf16[2048,1280]{0,1:T(8,128)(2,1)} %fusion.190, bf16[2,1280,4096]{2,1,0:T(8,128)(2,1)} %param.12, bf16[1,2048,4096]{2,1,0:T(8,128)(2,1)} %get-tuple-element.540), kind=kOutput, calls=%fused_computation.213 | convolution fusion | flops 21487941632 | bytes 42999808 | tf_op jit(solution)/vmap(transpose(jvp()))/dot_general | solution.py:20
  690.7 276.1 %while.17 = (bf16[1,2048,1280]{2,1,0:T(8,128)(2,1)}, bf16[1,2048,4096]{1,2,0:T(8,128)(2,1)}, f32[1280,256]{0,1:T(8,128)S(1)}, f32[1280,256]{0,1:T(8,128)}, u32[]...) while((bf16[1,2048,1280]{2,1,0:T(8,128)(2,1)}, ...), condition=%wide.windowed_dot_general_cond_rs.5.clone, body=%wide.windowed_dot_general_body_rs.5.clone.sunk | while | flops 5379063808 | bytes 91226696 | solution.py:9
  714.8 26.9 %collective-permute-start.22 = (f32[1280,256]{0,1:T(8,128)}, f32[1280,256]{0,1:T(8,128)}, u32[]{:S(2)}, u32[]{:S(2)}) collective-permute-start(f32[1280,256]{0,1:T(8,128)} %get-tuple-element.500), channel_id=37, source_target_pairs={{0,1},{1,2},{2,3},{3,4},{4,5},{5,6},{6,7},{7,8},{8,9},{9,10},{10,1... | collective-permute-start | bytes 3932168 | tf_op jit(solution)/vmap(transpose(jvp()))/dot_general | solution.py:9
  829.9 14.8 collective-permute-start.20
  899.5 14.8 collective-permute-start.20
  966.8 14.8 collective-permute-start.29
  993.0 328.3 %while.14 = (bf16[1,2048,4096]{2,1,0:T(8,128)(2,1)}, bf16[1,2048,1280]{1,2,0:T(8,128)(2,1)}, f32[4096,80]{0,1:T(8,128)S(1)}, f32[4096,80]{0,1:T(8,128)}, u32[]{:...) while((bf16[1,2048,4096]{2,1,0:T(8,128)(2,1)}, ...), condition=%wide.windowed_dot_general_cond_rs.2.clone, body=%wide.windowed_dot_general_body_rs.2.clone.sunk | while | flops 5373296640 | bytes 91226696 | solution.py:21
  1014.8 17.0 collective-permute-done.9
  1034.9 21.4 collective-permute-start.10
  1079.8 27.8 %collective-permute-start.8 = (f32[4096,80]{0,1:T(8,128)S(1)}, f32[4096,80]{0,1:T(8,128)}, u32[]{:S(2)}, u32[]{:S(2)}) collective-permute-start(f32[4096,80]{0,1:T(8,128)S(1)} %broadcast_select_fusion.28), channel_id=16, source_target_pairs={{0,1},{1,2},{2,3},{3,4},{4,5},{5,6},{6,7},{7,8},{8,9},{9,10},{10,1... | collective-permute-start | bytes 3932168 | tf_op jit(solution)/vmap(transpose(jvp()))/dot_general | solution.py:21
  1116.2 23.4 collective-permute-done.9
  1142.7 25.7 %collective-permute-start.10 = (f32[4096,80]{0,1:T(8,128)}, f32[4096,80]{0,1:T(8,128)S(1)}, u32[]{:S(2)}, u32[]{:S(2)}) collective-permute-start(f32[4096,80]{0,1:T(8,128)} %get-tuple-element.473), channel_id=18, source_target_pairs={{0,1},{1,2},{2,3},{3,4},{4,5},{5,6},{6,7},{7,8},{8,9},{9,10},{10,1... | collective-permute-start | bytes 3932168 | tf_op jit(solution)/vmap(transpose(jvp()))/dot_general | solution.py:21
  1254.4 14.8 collective-permute-start.8
  1321.3 14.8 collective-permute-start.26
  1336.1 48.3 %convert_multiply_fusion = (bf16[1,2048,4096]{2,1,0:T(8,128)(2,1)}, bf16[1,2048,4096]{2,1,0:T(8,128)(2,1)}) fusion(f32[2048,4096]{1,0:T(8,128)} %fusion.173, f32[2048,4096]{1,0:T(8,128)} %get-tuple-element.264, bf16[2,4096,1280]{2,1,0:T(8,128)(2,1)} %param.15, bf16[1,2048,1280]{1,2,0:T(8,128)(2,1)} %fusion.220), kind=kOutput, calls=%fused_computation.168 | convolution fusion | flops 21609054208 | bytes 116391936 | tf_op jit(solution)/vmap(transpose(jvp()))/dot_general | solution.py:9
  1384.4 276.2 %while.15 = (bf16[1,2048,4096]{2,1,0:T(8,128)(2,1)}, bf16[1,2048,1280]{1,2,0:T(8,128)(2,1)}, f32[4096,80]{0,1:T(8,128)S(1)}, f32[4096,80]{0,1:T(8,128)}, u32[]{:...) while((bf16[1,2048,4096]{2,1,0:T(8,128)(2,1)}, ...), condition=%wide.windowed_dot_general_cond_rs.3.clone, body=%wide.windowed_dot_general_body_rs.3.clone.sunk | while | flops 5373296640 | bytes 91226696 | solution.py:21
  1408.6 26.9 %collective-permute-start.14 = (f32[4096,80]{0,1:T(8,128)}, f32[4096,80]{0,1:T(8,128)}, u32[]{:S(2)}, u32[]{:S(2)}) collective-permute-start(f32[4096,80]{0,1:T(8,128)} %get-tuple-element.482), channel_id=24, source_target_pairs={{0,1},{1,2},{2,3},{3,4},{4,5},{5,6},{6,7},{7,8},{8,9},{9,10},{10,1... | collective-permute-start | bytes 3932168 | tf_op jit(solution)/vmap(transpose(jvp()))/dot_general | solution.py:21
  1593.4 14.8 collective-permute-start.12
  1686.8 330.1 %while.12 = (bf16[1,2048,4096]{2,1,0:T(8,128)(2,1)}, bf16[1,2048,1280]{1,2,0:T(8,128)(2,1)}, f32[4096,80]{0,1:T(8,128)S(1)}, f32[4096,80]{0,1:T(8,128)}, u32[]{:...) while((bf16[1,2048,4096]{2,1,0:T(8,128)(2,1)}, ...), condition=%wide.windowed_dot_general_cond_rs.clone, body=%wide.windowed_dot_general_body_rs.clone.sunk | while | flops 5373296640 | bytes 96469608 | solution.py:20
  1708.6 17.0 collective-permute-done.1
  1728.4 21.4 collective-permute-start.2
  1774.0 28.5 %collective-permute-start = (f32[4096,80]{0,1:T(8,128)S(1)}, f32[4096,80]{0,1:T(8,128)}, u32[]{:S(2)}, u32[]{:S(2)}) collective-permute-start(f32[4096,80]{0,1:T(8,128)S(1)} %broadcast_select_fusion.24), channel_id=3, source_target_pairs={{0,1},{1,2},{2,3},{3,4},{4,5},{5,6},{6,7},{7,8},{8,9},{9,10},{10,1... | collective-permute-start | bytes 3932168 | tf_op jit(solution)/vmap(transpose(jvp()))/dot_general | solution.py:20
  1811.2 22.5 collective-permute-done.1
  1836.4 25.1 %collective-permute-start.2 = (f32[4096,80]{0,1:T(8,128)}, f32[4096,80]{0,1:T(8,128)S(1)}, u32[]{:S(2)}, u32[]{:S(2)}) collective-permute-start(f32[4096,80]{0,1:T(8,128)} %get-tuple-element.455), channel_id=5, source_target_pairs={{0,1},{1,2},{2,3},{3,4},{4,5},{5,6},{6,7},{7,8},{8,9},{9,10},{10,1... | collective-permute-start | bytes 3932168 | tf_op jit(solution)/vmap(transpose(jvp()))/dot_general | solution.py:20
  1949.0 15.9 collective-permute-start
  2016.9 15.9 collective-permute-start.24
  2032.8 276.8 %while.13 = (bf16[1,2048,4096]{2,1,0:T(8,128)(2,1)}, bf16[1,2048,1280]{1,2,0:T(8,128)(2,1)}, f32[4096,80]{0,1:T(8,128)S(1)}, f32[4096,80]{0,1:T(8,128)}, u32[]{:...) while((bf16[1,2048,4096]{2,1,0:T(8,128)(2,1)}, ...), condition=%wide.windowed_dot_general_cond_rs.1.clone, body=%wide.windowed_dot_general_body_rs.1.clone.sunk | while | flops 5373296640 | bytes 91226696 | solution.py:20
  2056.9 26.9 %collective-permute-start.6 = (f32[4096,80]{0,1:T(8,128)}, f32[4096,80]{0,1:T(8,128)}, u32[]{:S(2)}, u32[]{:S(2)}) collective-permute-start(f32[4096,80]{0,1:T(8,128)} %get-tuple-element.464), channel_id=11, source_target_pairs={{0,1},{1,2},{2,3},{3,4},{4,5},{5,6},{6,7},{7,8},{8,9},{9,10},{10,1... | collective-permute-start | bytes 3932168 | tf_op jit(solution)/vmap(transpose(jvp()))/dot_general | solution.py:20
  2334.4 103.9 %all-gather.10.cloned.1.call-done = bf16[1,2,1280,4096]{3,2,1,0:T(8,128)(2,1)} async-done(((bf16[1,2,80,4096]{3,2,1,0:T(8,128)(2,1)}), bf16[1,2,1280,4096]{3,2,1,0:T(8,128)(2,1)}) %all-gather.10.cloned.1.call-update) | async-done | bytes 20971536 | tf_op jit(solution)/reshape | solution.py:52
  2438.3 21.1 copy.63
  (429 shorter events, 1406.7 us)
Async XLA Ops:
  7.2 2327.2 %all-gather.14.cloned.1.call-start = ((), (), s32[]{:S(2)}) async-start(), calls=%async_computation.2 | async-start | bytes 22282240 | tf_op jit(solution)/reshape | solution.py:52
  316.5 32.9 %collective-permute-start.18 = (f32[256,1280]{1,0:T(8,128)}, f32[256,1280]{1,0:T(8,128)S(1)}, u32[]{:S(2)}, u32[]{:S(2)}) collective-permute-start(f32[256,1280]{1,0:T(8,128)} %get-tuple-element.491), channel_id=31, source_target_pairs={{0,1},{1,2},{2,3},{3,4},{4,5},{5,6},{6,7},{7,8},{8,9},{9,10},{10,1... | collective-permute-start | bytes 3932168 | tf_op jit(solution)/vmap(transpose(jvp()))/dot_general | solution.py:9
  395.5 20.8 collective-permute-start.18
  429.5 22.1 collective-permute-start.16
  497.9 21.9 collective-permute-start.16
  564.8 416.9 %collective-permute-start.28 = (f32[256,1280]{1,0:T(8,128)}, f32[256,1280]{1,0:T(8,128)}, u32[]{:S(2)}, u32[]{:S(2)}) collective-permute-start(f32[256,1280]{1,0:T(8,128)} %get-tuple-element.45), channel_id=32, source_target_pairs={{0,1},{1,2},{2,3},{3,4},{4,5},{5,6},{6,7},{7,8},{8,9},{9,10},{10,1... | collective-permute-start | bytes 3932168 | tf_op jit(solution)/vmap(transpose(jvp()))/dot_general | solution.py:9
  714.8 32.9 %collective-permute-start.22 = (f32[1280,256]{0,1:T(8,128)}, f32[1280,256]{0,1:T(8,128)}, u32[]{:S(2)}, u32[]{:S(2)}) collective-permute-start(f32[1280,256]{0,1:T(8,128)} %get-tuple-element.500), channel_id=37, source_target_pairs={{0,1},{1,2},{2,3},{3,4},{4,5},{5,6},{6,7},{7,8},{8,9},{9,10},{10,1... | collective-permute-start | bytes 3932168 | tf_op jit(solution)/vmap(transpose(jvp()))/dot_general | solution.py:9
  829.9 21.9 collective-permute-start.20
  864.0 20.8 collective-permute-start.22
  899.5 22.0 collective-permute-start.20
  992.9 1341.5 %all-gather.12.cloned.1.call-start = ((), (), s32[]{:S(2)}) async-start(), calls=%async_computation.1 | async-start | bytes 22282240 | tf_op jit(solution)/reshape | solution.py:52
  993.3 21.5 collective-permute-start.8
  1007.3 24.6 collective-permute-start.9
  1034.9 33.2 %collective-permute-start.10 = (f32[4096,80]{0,1:T(8,128)}, f32[4096,80]{0,1:T(8,128)S(1)}, u32[]{:S(2)}, u32[]{:S(2)}) collective-permute-start(f32[4096,80]{0,1:T(8,128)} %get-tuple-element.473), channel_id=18, source_target_pairs={{0,1},{1,2},{2,3},{3,4},{4,5},{5,6},{6,7},{7,8},{8,9},{9,10},{10,1... | collective-permute-start | bytes 3932168 | tf_op jit(solution)/vmap(transpose(jvp()))/dot_general | solution.py:21
  1079.8 36.4 %collective-permute-start.8 = (f32[4096,80]{0,1:T(8,128)S(1)}, f32[4096,80]{0,1:T(8,128)}, u32[]{:S(2)}, u32[]{:S(2)}) collective-permute-start(f32[4096,80]{0,1:T(8,128)S(1)} %broadcast_select_fusion.28), channel_id=16, source_target_pairs={{0,1},{1,2},{2,3},{3,4},{4,5},{5,6},{6,7},{7,8},{8,9},{9,10},{10,1... | collective-permute-start | bytes 3932168 | tf_op jit(solution)/vmap(transpose(jvp()))/dot_general | solution.py:21
  1108.7 30.9 %collective-permute-start.9 = (f32[4096,80]{0,1:T(8,128)}, f32[4096,80]{0,1:T(8,128)}, u32[]{:S(2)}, u32[]{:S(2)}) collective-permute-start(f32[4096,80]{0,1:T(8,128)} %broadcast_select_fusion.29), channel_id=15, source_target_pairs={{0,15},{1,0},{2,1},{3,2},{4,3},{5,4},{6,5},{7,6},{8,7},{9,8},{10,9... | collective-permute-start | bytes 3932168 | tf_op jit(solution)/vmap(transpose(jvp()))/dot_general | solution.py:21
  1142.7 33.2 %collective-permute-start.10 = (f32[4096,80]{0,1:T(8,128)}, f32[4096,80]{0,1:T(8,128)S(1)}, u32[]{:S(2)}, u32[]{:S(2)}) collective-permute-start(f32[4096,80]{0,1:T(8,128)} %get-tuple-element.473), channel_id=18, source_target_pairs={{0,1},{1,2},{2,3},{3,4},{4,5},{5,6},{6,7},{7,8},{8,9},{9,10},{10,1... | collective-permute-start | bytes 3932168 | tf_op jit(solution)/vmap(transpose(jvp()))/dot_general | solution.py:21
  1187.7 22.1 collective-permute-start.8
  1220.6 22.0 collective-permute-start.10
  1254.4 23.5 collective-permute-start.8
  1288.6 22.3 collective-permute-start.10
  1321.3 354.1 %collective-permute-start.26 = (f32[4096,80]{0,1:T(8,128)}, f32[4096,80]{0,1:T(8,128)}, u32[]{:S(2)}, u32[]{:S(2)}) collective-permute-start(f32[4096,80]{0,1:T(8,128)} %get-tuple-element.41), channel_id=19, source_target_pairs={{0,1},{1,2},{2,3},{3,4},{4,5},{5,6},{6,7},{7,8},{8,9},{9,10},{10,1... | collective-permute-start | bytes 3932168 | tf_op jit(solution)/vmap(transpose(jvp()))/dot_general | solution.py:21
  1408.6 34.4 %collective-permute-start.14 = (f32[4096,80]{0,1:T(8,128)}, f32[4096,80]{0,1:T(8,128)}, u32[]{:S(2)}, u32[]{:S(2)}) collective-permute-start(f32[4096,80]{0,1:T(8,128)} %get-tuple-element.482), channel_id=24, source_target_pairs={{0,1},{1,2},{2,3},{3,4},{4,5},{5,6},{6,7},{7,8},{8,9},{9,10},{10,1... | collective-permute-start | bytes 3932168 | tf_op jit(solution)/vmap(transpose(jvp()))/dot_general | solution.py:21
  1456.2 22.1 collective-permute-start.12
  1489.0 21.4 collective-permute-start.14
  1523.7 23.4 collective-permute-start.12
  1557.8 22.3 collective-permute-start.14
  1593.4 23.5 collective-permute-start.12
  1627.6 22.3 collective-permute-start.14
  1686.7 751.5 %all-gather.10.cloned.1.call-start = ((), (), s32[]{:S(2)}) async-start(), calls=%async_computation | async-start | bytes 22282240 | tf_op jit(solution)/reshape | solution.py:52
  1687.1 21.5 collective-permute-start
  1701.1 24.6 collective-permute-start.1
  1728.4 32.5 %collective-permute-start.2 = (f32[4096,80]{0,1:T(8,128)}, f32[4096,80]{0,1:T(8,128)S(1)}, u32[]{:S(2)}, u32[]{:S(2)}) collective-permute-start(f32[4096,80]{0,1:T(8,128)} %get-tuple-element.455), channel_id=5, source_target_pairs={{0,1},{1,2},{2,3},{3,4},{4,5},{5,6},{6,7},{7,8},{8,9},{9,10},{10,1... | collective-permute-start | bytes 3932168 | tf_op jit(solution)/vmap(transpose(jvp()))/dot_general | solution.py:20
  1774.0 37.1 %collective-permute-start = (f32[4096,80]{0,1:T(8,128)S(1)}, f32[4096,80]{0,1:T(8,128)}, u32[]{:S(2)}, u32[]{:S(2)}) collective-permute-start(f32[4096,80]{0,1:T(8,128)S(1)} %broadcast_select_fusion.24), channel_id=3, source_target_pairs={{0,1},{1,2},{2,3},{3,4},{4,5},{5,6},{6,7},{7,8},{8,9},{9,10},{10,1... | collective-permute-start | bytes 3932168 | tf_op jit(solution)/vmap(transpose(jvp()))/dot_general | solution.py:20
  1803.6 30.0 %collective-permute-start.1 = (f32[4096,80]{0,1:T(8,128)}, f32[4096,80]{0,1:T(8,128)S(1)}, u32[]{:S(2)}, u32[]{:S(2)}) collective-permute-start(f32[4096,80]{0,1:T(8,128)} %broadcast_select_fusion.25), channel_id=2, source_target_pairs={{0,15},{1,0},{2,1},{3,2},{4,3},{5,4},{6,5},{7,6},{8,7},{9,8},{10,9... | collective-permute-start | bytes 3932168 | tf_op jit(solution)/vmap(transpose(jvp()))/dot_general | solution.py:20
  1836.4 32.6 %collective-permute-start.2 = (f32[4096,80]{0,1:T(8,128)}, f32[4096,80]{0,1:T(8,128)S(1)}, u32[]{:S(2)}, u32[]{:S(2)}) collective-permute-start(f32[4096,80]{0,1:T(8,128)} %get-tuple-element.455), channel_id=5, source_target_pairs={{0,1},{1,2},{2,3},{3,4},{4,5},{5,6},{6,7},{7,8},{8,9},{9,10},{10,1... | collective-permute-start | bytes 3932168 | tf_op jit(solution)/vmap(transpose(jvp()))/dot_general | solution.py:20
  1881.2 23.2 collective-permute-start
  1914.7 22.0 collective-permute-start.2
  1949.0 24.5 collective-permute-start
  1983.9 22.3 collective-permute-start.2
  2016.9 307.5 %collective-permute-start.24 = (f32[4096,80]{0,1:T(8,128)}, f32[4096,80]{0,1:T(8,128)}, u32[]{:S(2)}, u32[]{:S(2)}) collective-permute-start(f32[4096,80]{0,1:T(8,128)} %get-tuple-element.37), channel_id=6, source_target_pairs={{0,1},{1,2},{2,3},{3,4},{4,5},{5,6},{6,7},{7,8},{8,9},{9,10},{10,1... | collective-permute-start | bytes 3932168 | tf_op jit(solution)/vmap(transpose(jvp()))/dot_general | solution.py:20
  2056.9 34.4 %collective-permute-start.6 = (f32[4096,80]{0,1:T(8,128)}, f32[4096,80]{0,1:T(8,128)}, u32[]{:S(2)}, u32[]{:S(2)}) collective-permute-start(f32[4096,80]{0,1:T(8,128)} %get-tuple-element.464), channel_id=11, source_target_pairs={{0,1},{1,2},{2,3},{3,4},{4,5},{5,6},{6,7},{7,8},{8,9},{9,10},{10,1... | collective-permute-start | bytes 3932168 | tf_op jit(solution)/vmap(transpose(jvp()))/dot_general | solution.py:20
  2104.6 22.1 collective-permute-start.4
  2137.4 22.0 collective-permute-start.6
  2172.6 23.4 collective-permute-start.4
  2206.8 22.3 collective-permute-start.6
  2242.3 23.4 collective-permute-start.4
  2276.5 22.3 collective-permute-start.6
  (90 other events, 1971.2 us)
Sparse Core Ops, SparseCore 0:
  993.0 172.7 all-gather.13
  1686.9 171.6 all-gather.11
  2334.5 103.7 all-gather.9
where the time goes:
time: 2500 us; the launch traced here: 2490 us
  starting transfers between devices  853 us (34%)
  matrix products  657 us (26%)
  waiting for transfers between devices  556 us (22%)
  other arithmetic  285 us (11%)
  local copies, waits for them, and re-layouts  121 us (5%)
    dot_general x34, starting transfers between devices, layer(): gate = jnp.dot(a, w['w_gate'], preferred_element_type=jnp.float32)  296 us
    dot_general x34, starting transfers between devices, layer(): up = jnp.dot(a, w['w_up'], preferred_element_type=jnp.float32)  292 us
    dot_general x34, starting transfers between devices, matmul(): jnp.dot(a, w, preferred_element_type=jnp.float32).astype(jnp.bfloat16)  266 us
    dot_general x19, matrix products, layer(): gate = jnp.dot(a, w['w_gate'], preferred_element_type=jnp.float32)  234 us
    dot_general x19, matrix products, layer(): up = jnp.dot(a, w['w_up'], preferred_element_type=jnp.float32)  219 us
    dot_general x19, matrix products, matmul(): jnp.dot(a, w, preferred_element_type=jnp.float32).astype(jnp.bfloat16)  204 us
    dot_general x34, waiting for transfers between devices, layer(): up = jnp.dot(a, w['w_up'], preferred_element_type=jnp.float32)  154 us
    dot_general x34, waiting for transfers between devices, layer(): gate = jnp.dot(a, w['w_gate'], preferred_element_type=jnp.float32)  149 us
  transfers between devices with their start and end apart: 105, of which 58 were waited for; matrix products, arithmetic and copies ran while one was open for 28% of the time, Pallas kernels for 0%

commit v1 on v0

v1 whole, which is shorter than its diff:
```python
import itertools

import jax
import jax.numpy as jnp
from jax import lax
from jax.experimental import pallas as pl
from jax.experimental.pallas import tpu as pltpu
from jax.sharding import PartitionSpec as P

F32, BF16 = jnp.float32, jnp.bfloat16
T, D, FF = 2048, 1280, 4096
N = 16
TILE = 256
ROWS = D // N
ORDERS = ((0, 1, 2), (1, 2, 0), (2, 0, 1))


def params():
    return pltpu.CompilerParams(vmem_limit_bytes=64_000_000)


def cost(flops, nbytes):
    return pl.CostEstimate(flops=int(flops), bytes_accessed=int(nbytes), transcendentals=0)


def dot(a, b, ca, cb):
    return lax.dot_general(a, b, (((ca,), (cb,)), ((), ())), preferred_element_type=F32)


def shape(dims, dtype):
    return jax.ShapeDtypeStruct(dims, dtype)


def normed(wide):
    scale = lax.rsqrt(jnp.mean(wide**2, -1, keepdims=True) + 1e-6)
    return (wide * scale).astype(BF16)


def in_order(j, order):
    x, y, z = (j >> 2) & 1, (j >> 1) & 1, j & 1
    a, b, c = ((x, y, z)[axis] for axis in order)
    return (a << 2) | (b << 1) | c


def within(i, start, count):
    return jnp.clip(i - start, 0, count - 1)


def block_of(j, d, other):
    return ((j ^ (d >> 1)) << 1) | ((d & 1) ^ other)


PARTNERS = (1, 2, 4, 8)
IDS = itertools.count()


def ride(load, keep, came, out, sems, event):
    here = lax.axis_index("dp")
    local, sent, received = sems

    def exchange(p, k):
        bit = 1 if k == 0 else 8 >> ORDERS[p][k - 1]
        source = load[0][p] if k == 0 else keep[p].at[pl.ds(8 >> k, 8 >> k)]
        return pltpu.make_async_remote_copy(
            src_ref=source,
            dst_ref=came[p][k],
            send_sem=sent.at[4 * p + k],
            recv_sem=received.at[4 * p + k],
            device_id={"dp": here ^ bit},
            device_id_type=pl.DeviceIdType.MESH,
        )

    def own(p):
        return pltpu.make_async_copy(load[1][p], keep[p], local.at[p])

    if event == 0:
        for p in range(3):
            exchange(p, 0).start()
        for p in range(3):
            own(p).start()
        return
    for p in range(3):
        if event == 1:
            own(p).wait()
        exchange(p, event - 1).wait_recv()
    if event < 4:
        count = 8 >> event
        for p in range(3):

            @pl.loop(count, 2 * count)
            def _(b):
                total = keep[p][b].astype(F32)
                for k in range(event):
                    total = total + came[p][k][b].astype(F32)
                keep[p][b] = total.astype(BF16)

        for p in range(3):
            exchange(p, event).start()
        return
    at = 0
    for p in range(3):
        total = keep[p][0].astype(F32)
        for k in range(4):
            total = total + came[p][k][0].astype(F32)
        out[:, at : at + total.shape[1]] = total.astype(BF16)
        at += total.shape[1]
        for k in range(4):
            exchange(p, k).wait_send()


def call(body, steps, ins, outs, args, riders=(), scratch=(), flops=0, nbytes=0, aliases=None, name=None):
    n_in, n_out, n_scratch, n = len(ins), len(outs), len(scratch), len(riders)
    events = [0, max(1, round(0.2 * steps)), round(0.55 * steps), round(0.8 * steps)]

    def whole(*refs):
        refs = list(refs)

        def take(count):
            some = refs[:count]
            del refs[:count]
            return some

        own_in = take(n_in)
        loads = [(take(3), take(3)) for _ in riders]
        own_out = take(n_out)
        sums = take(n)
        own_scratch = take(n_scratch)
        rides = []
        for q in range(n):
            keep = take(3)
            came = [take(4) for _ in range(3)]
            rides.append((loads[q], keep, came, sums[q], take(3)))
        i = pl.program_id(0)
        if n:

            def go(event):
                if event == 0:
                    here = lax.axis_index("dp")
                    barrier = pltpu.get_barrier_semaphore()
                    for bit in PARTNERS:
                        pl.semaphore_signal(barrier, inc=1, device_id={"dp": here ^ bit}, device_id_type=pl.DeviceIdType.MESH)
                    pl.semaphore_wait(barrier, len(PARTNERS))
                for one in rides:
                    ride(*one, event)

            for event in range(4):
                if steps == 1:
                    go(event)
                else:
                    pl.when(i == events[event])(lambda event=event: go(event))

        if body is not None:
            body(*own_in, *own_out, *own_scratch)

        if n:
            if steps == 1:
                go(4)
            else:
                pl.when(i == steps - 1)(lambda: go(4))

    ride_scratch, sum_outs, extra = [], [], {}
    for send, keep in riders:
        rows = keep[0].shape[1]
        ride_scratch += [pltpu.VMEM(t.shape, BF16) for t in keep]
        for t in keep:
            ride_scratch += [pltpu.VMEM((count, *t.shape[1:]), BF16) for count in (8, 4, 2, 1)]
        ride_scratch += [pltpu.SemaphoreType.DMA((3,)), pltpu.SemaphoreType.DMA((12,)), pltpu.SemaphoreType.DMA((12,))]
        form = (rows, sum(t.shape[2] for t in keep))
        sum_outs.append((pl.BlockSpec(form, lambda i: (0, 0)), shape(form, BF16)))
        extra = {"has_side_effects": True}
    if riders:
        extra["collective_id"] = next(IDS)
    outs = list(outs) + sum_outs
    result = pl.pallas_call(
        whole,
        grid=(steps,),
        in_specs=list(ins) + [pl.BlockSpec(memory_space=pl.ANY)] * (6 * n),
        out_specs=[spec for spec, _ in outs],
        out_shape=[form for _, form in outs],
        scratch_shapes=list(scratch) + ride_scratch,
        input_output_aliases=aliases or {},
        compiler_params=pltpu.CompilerParams(vmem_limit_bytes=66_000_000, **extra),
        cost_estimate=cost(flops, nbytes),
        name=name,
    )(*args, *[t for send, keep in riders for t in (*send, *keep)])
    return list(result[:n_out]), list(result[n_out:])


def forward(a, w_gate, w_up, number):
    def body(a, wg, wu, act, gate, up):
        g = dot(a[...], wg[...], 1, 0)
        u = dot(a[...], wu[...], 1, 0)
        gate[...] = g
        up[...] = u
        act[...] = (jax.nn.silu(g) * u).astype(BF16)

    tile = pl.BlockSpec((T, TILE), lambda j: (0, j))
    w = pl.BlockSpec((None, D, TILE), lambda j: (number, 0, j))
    return pl.pallas_call(
        body,
        grid=(FF // TILE,),
        in_specs=[pl.BlockSpec((T, D), lambda j: (0, 0)), w, w],
        out_specs=[tile] * 3,
        out_shape=[shape((T, FF), BF16), shape((T, FF), F32), shape((T, FF), F32)],
        compiler_params=params(),
        cost_estimate=cost(4 * T * D * FF, 140e6),
        name="forward",
    )(a, w_gate, w_up)


def prepare(x):
    rows = 256

    def body(x, a, at):
        new = normed(x[...].astype(F32))
        a[...] = new
        at[...] = new.T

    some = pl.BlockSpec((rows, D), lambda i: (i, 0))
    return pl.pallas_call(
        body,
        grid=(T // rows,),
        in_specs=[some],
        out_specs=[some, pl.BlockSpec((D, rows), lambda i: (0, i))],
        out_shape=[shape((T, D), BF16), shape((D, T), BF16)],
        compiler_params=params(),
        cost_estimate=cost(1e8, 16e6),
        name="prepare",
    )(x)


def down(act, h, w_down, number):
    rows = 256

    def body(act, h, w, out, a, at):
        new = h[...] + dot(act[...], w[...], 1, 0).astype(BF16)
        out[...] = new
        new = normed(new.astype(F32))
        a[...] = new
        at[...] = new.T

    some = pl.BlockSpec((rows, D), lambda i: (i, 0))
    return pl.pallas_call(
        body,
        grid=(T // rows,),
        in_specs=[
            pl.BlockSpec((rows, FF), lambda i: (i, 0)),
            some,
            pl.BlockSpec((None, FF, D), lambda i: (number, 0, 0), pipeline_mode=pl.Buffered(1)),
        ],
        out_specs=[some, some, pl.BlockSpec((D, rows), lambda i: (0, i))],
        out_shape=[shape((T, D), BF16)] * 2 + [shape((D, T), BF16)],
        compiler_params=params(),
        cost_estimate=cost(2 * T * D * FF, 40e6),
        name="down",
    )(act, h, w_down)


def gradients_in(at, rows, held, outs, sems, tiles, parts):
    half = N // 2
    i = pl.program_id(0)
    here = lax.axis_index("dp")
    starts = [sum(parts[:p]) for p in range(3)]
    loads = [
        pltpu.make_async_copy(
            at.at[block_of(j & 7, here, 1 - (j >> 3))], rows.at[pl.ds(j * ROWS, ROWS)], sems[0].at[j]
        )
        for j in range(N)
    ]
    each = tiles // (len(held) // 6)
    puts = [pltpu.make_async_copy(held[k], outs[k], sems[1].at[k]) for k in range(len(held))]

    def begin():
        @pl.when(i == 0)
        def _():
            for load in loads:
                load.start()

    def finish(by_gate, by_up):
        @pl.when(i == 0)
        def _():
            for load in loads:
                load.wait()

        both = dot(rows[...], jnp.concatenate([by_gate, by_up], axis=1), 1, 0).astype(BF16)
        for step in range(tiles):

            @pl.when(i == step)
            def _():
                unit = step // each
                for which in range(2):
                    t = which * each + step % each
                    p = max(q for q in range(3) if starts[q] <= t)
                    columns = slice((t - starts[p]) * TILE, (t - starts[p] + 1) * TILE)
                    new = both[:, which * TILE : (which + 1) * TILE]
                    for k in range(2):
                        for j in range(half):
                            row = (k * half + j) * ROWS
                            held[6 * unit + 3 * k + p][in_order(j, ORDERS[p]), :, columns] = new[row : row + ROWS]
                if (step + 1) % each == 0:
                    for put in puts[6 * unit : 6 * unit + 6]:
                        put.start()

        @pl.when(i == tiles - 1)
        def _():
            for put in puts:
                put.wait()

    return begin, finish


def gradient_forms(units, parts):
    half = N // 2
    forms = [(half, ROWS, parts[p] * TILE) for unit in range(units) for k in range(2) for p in range(3)]
    outs = [(pl.BlockSpec(memory_space=pl.ANY), shape(form, BF16)) for form in forms]
    scratch = [pltpu.VMEM((D, T), BF16)] + [pltpu.VMEM(form, BF16) for form in forms]
    return outs, scratch + [pltpu.SemaphoreType.DMA((N,)), pltpu.SemaphoreType.DMA((6 * units,))]


def back(g, u, c):
    c = c.astype(BF16).astype(F32)
    sig = jax.nn.sigmoid(g)
    silu = g * sig
    return (silu * u).astype(BF16), (c * u * (sig * (1 + g * (1 - sig)))).astype(BF16), (c * silu).astype(BF16)


def last_layer(riders, a, at, dy, w_gate, w_up, w_down, number, first, tiles, parts, so_far):
    n = len(so_far)

    def body(a, dy, wg, wu, wd, at, *refs):
        refs = refs[n:]
        dgate, dup, act = refs[:3]
        outs, (rows, *held, loaded, put) = refs[3:9], refs[9:]
        begin, finish = gradients_in(at, rows, held, outs, (loaded, put), tiles, parts)
        begin()
        g = dot(a[...], wg[...], 1, 0)
        u = dot(a[...], wu[...], 1, 0)
        act[...], dgate[...], dup[...] = back(g, u, dot(dy[...], wd[...], 1, 1))
        finish(dgate[...], dup[...])

    full = pl.BlockSpec((T, D), lambda j: (0, 0), pipeline_mode=pl.Buffered(1))
    tile = pl.BlockSpec((T, TILE), lambda j: (0, first + j))
    w = pl.BlockSpec((None, D, TILE), lambda j: (number, 0, first + j))
    wd = pl.BlockSpec((None, TILE, D), lambda j: (number, first + j, 0))
    anywhere = pl.BlockSpec(memory_space=pl.ANY)
    outs, scratch = gradient_forms(1, parts)
    outs, sums = call(
        body,
        tiles,
        [full, full, w, w, wd, anywhere] + [anywhere] * n,
        [(tile, shape((T, FF), BF16))] * 3 + outs,
        (a, dy, w_gate, w_up, w_down, at, *so_far),
        riders,
        scratch=scratch,
        aliases={6: 0, 7: 1, 8: 2} if so_far else {},
        flops=10 * T * D * TILE * tiles,
        nbytes=8e6 * tiles,
        name="last_layer",
    )
    return (outs[:3], (outs[3:6], outs[6:])), sums


def first_layer(riders, dh, at, gate, up, w_down, number, first, units, parts):
    tiles = units * TILES

    def body(dh, g, u, wd, at, *refs):
        outs, (rows, *held, loaded, put) = refs[: 6 * units], refs[6 * units :]
        begin, finish = gradients_in(at, rows, held, outs, (loaded, put), tiles, parts)
        begin()
        _, dgate, dup = back(g[...], u[...], dot(dh[...], wd[...], 1, 1))
        finish(dgate, dup)

    full = pl.BlockSpec((T, D), lambda j: (0, 0), pipeline_mode=pl.Buffered(1))
    kept = pl.BlockSpec((T, TILE), lambda j: (0, first + j))
    wd = pl.BlockSpec((None, TILE, D), lambda j: (number, first + j, 0))
    outs, scratch = gradient_forms(units, parts)
    outs, sums = call(
        body,
        tiles,
        [full, kept, kept, wd, pl.BlockSpec(memory_space=pl.ANY)],
        outs,
        (dh, gate, up, w_down, at),
        riders,
        scratch=scratch,
        flops=6 * T * D * TILE * tiles,
        nbytes=8e6 * tiles,
        name="first_layer",
    )
    return [(outs[k : k + 3], outs[k + 3 : k + 6]) for k in range(0, 6 * units, 6)], sums


def gradient_out(riders, act, dy, parts):
    half = N // 2
    starts = [128 * sum(parts[:p]) for p in range(3)]
    rows = TILE // 2

    def body(act, dy, *outs):
        new = dot(act[...], dy[...], 0, 0).astype(BF16)
        for k in range(2):

            @pl.when((pl.program_id(0) >> 3) == k)
            def _():
                for q in range(2):
                    for p in range(3):
                        columns = slice(starts[p], starts[p] + 128 * parts[p])
                        outs[6 * q + 3 * k + p][...] = new[q * rows : (q + 1) * rows, columns]

    def out_spec(k, p):
        return pl.BlockSpec((None, rows, 128 * parts[p]), lambda i: (in_order(within(i, k * half, half), ORDERS[p]), 0, 0))

    outs, sums = call(
        body,
        N,
        [
            pl.BlockSpec((T, TILE), lambda i: (0, block_of(i & 7, lax.axis_index("dp"), 1 - (i >> 3)))),
            pl.BlockSpec((T, D), lambda i: (0, 0), pipeline_mode=pl.Buffered(1)),
        ],
        [(out_spec(k, p), shape((half, rows, 128 * parts[p]), BF16)) for q in range(2) for k in range(2) for p in range(3)],
        (act, dy),
        riders,
        flops=2 * T * D * FF,
        nbytes=33e6,
        name="gradient_out",
    )
    return [(outs[:3], outs[3:6]), (outs[6:9], outs[9:])], sums


def states_backward(riders, dgate, dup, w_gate, w_up, h, dy, number):
    wide = 512

    def body(dg, du, wg, wu, h, dy, out, by_gate, by_up, states, sem):
        i = pl.program_id(0)
        load = pltpu.make_async_copy(h, states, sem.at[0])
        put = pltpu.make_async_copy(states, out, sem.at[1])

        @pl.when(i == 0)
        def _():
            load.start()
            by_gate[...] = dot(dg[...], wg[...], 1, 1)
            by_up[...] = dot(du[...], wu[...], 1, 1)

        @pl.when(i > 0)
        def _():
            by_gate[...] += dot(dg[...], wg[...], 1, 1)
            by_up[...] += dot(du[...], wu[...], 1, 1)

        @pl.when(i == FF // wide - 1)
        def _():
            rows = 256
            load.wait()

            @pl.loop(0, T // rows)
            def _(r):
                at = pl.ds(pl.multiple_of(r * rows, rows), rows)
                da = (by_gate[at, :].astype(BF16) + by_up[at, :].astype(BF16)).astype(F32)
                x = states[at, :].astype(F32)
                scale = lax.rsqrt(jnp.mean(x**2, -1, keepdims=True) + 1e-6)
                along = jnp.mean(da * x, -1, keepdims=True)
                dx = da * scale - x * (scale**3 * along)
                states[at, :] = dy[at, :] + dx.astype(BF16)

            put.start()
            put.wait()

    full = pl.BlockSpec((T, D), lambda i: (0, 0), pipeline_mode=pl.Buffered(1))
    anywhere = pl.BlockSpec(memory_space=pl.ANY)
    tile = pl.BlockSpec((T, wide), lambda i: (0, i))
    w = pl.BlockSpec((None, D, wide), lambda i: (number, 0, i))
    (out,), sums = call(
        body,
        FF // wide,
        [tile, tile, w, w, anywhere, full],
        [(anywhere, shape((T, D), BF16))],
        (dgate, dup, w_gate, w_up, h, dy),
        riders,
        scratch=[pltpu.VMEM((T, D), F32)] * 2 + [pltpu.VMEM((T, D), BF16), pltpu.SemaphoreType.DMA((2,))],
        flops=4 * T * D * FF,
        nbytes=70e6,
        name="states_backward",
    )
    return out, sums


def update_in(place, sums, w_gate, w_up, m, v, number, first, tiles):
    steps, wide = 5, tiles * TILE
    rows, n = ROWS // steps, len(sums)

    def body(s, *refs):
        new, at = refs[-1], 0
        for q in range(n):
            for k in range(2):
                w, m, v = refs[n + 3 * (2 * q + k) :][:3]
                g = refs[q][:, k * wide : (k + 1) * wide]
                new[:, at : at + wide] = new_weight(w[...], m[...], v[...], g)
                at += wide

    def state(q):
        return pl.BlockSpec((None, rows, wide), lambda i, s: (number, i, first // tiles + q))

    def own(q):
        return pl.BlockSpec((None, rows, wide), lambda i, s: (number, s[0] * steps + i, first // tiles + q))

    return pl.pallas_call(
        body,
        grid_spec=pltpu.PrefetchScalarGridSpec(
            num_scalar_prefetch=1,
            grid=(steps,),
            in_specs=[pl.BlockSpec((rows, 2 * wide), lambda i, s: (i, 0))] * n
            + [spec for q in range(n) for _ in range(2) for spec in (own(q), state(q), state(q))],
            out_specs=pl.BlockSpec((rows, 2 * n * wide), lambda i, s: (i, 0)),
        ),
        out_shape=shape((ROWS, 2 * n * wide), BF16),
        compiler_params=params(),
        cost_estimate=cost(1e8, 1e7),
        name="update_in",
    )(place, *sums, *[t for q in range(n) for one in zip((w_gate, w_up), m, v) for t in one])


def update_out(place, sums, w_down, m, v, number):
    rows = TILE // 2

    def body(s, one, two, w, m, v, new):
        for q, g in enumerate((one, two)):

            @pl.when(pl.program_id(0) == q)
            def _():
                new[...] = new_weight(w[...], m[...], v[...], g[...])

    whole = pl.BlockSpec((rows, D), lambda i, s: (0, 0))
    state = pl.BlockSpec((None, rows, D), lambda i, s: (number, i, 0))
    own = pl.BlockSpec((None, rows, D), lambda i, s: (number, s[0] * 2 + i, 0))
    return pl.pallas_call(
        body,
        grid_spec=pltpu.PrefetchScalarGridSpec(
            num_scalar_prefetch=1,
            grid=(2,),
            in_specs=[whole, whole, own, state, state],
            out_specs=pl.BlockSpec((rows, D), lambda i, s: (i, 0)),
        ),
        out_shape=shape((TILE, D), BF16),
        compiler_params=params(),
        cost_estimate=cost(1e8, 1e7),
        name="update_out",
    )(place, *sums, w_down, m, v)


def lay_in(gathered, outs, number, first, tiles):
    wide, rows = 512, 640
    each = tiles * TILE // wide
    blocks = gathered.shape[1] // 2 // wide

    def body(gate, up, *refs):
        refs[-2][...] = gate[...]
        refs[-1][...] = up[...]

    out = pl.BlockSpec((None, rows, wide), lambda i, j: (number, i, first * TILE // wide + j))
    return pl.pallas_call(
        body,
        grid=(D // rows, blocks),
        in_specs=[
            pl.BlockSpec((rows, wide), lambda i, j: (i, (j // each) * 2 * each + j % each)),
            pl.BlockSpec((rows, wide), lambda i, j: (i, (j // each) * 2 * each + each + j % each)),
        ]
        + [pl.BlockSpec(memory_space=pl.ANY)] * len(outs),
        out_specs=[out, out],
        out_shape=[shape((2, D, FF), BF16)] * 2,
        input_output_aliases={2: 0, 3: 1} if outs else {},
        compiler_params=params(),
        cost_estimate=cost(1e8, 2e7),
        name="lay_in",
    )(gathered, gathered, *outs)


def lay_out(gathered, outs, number):
    rows = 512

    def body(new, *refs):
        refs[-1][...] = new[...]

    return pl.pallas_call(
        body,
        grid=(FF // rows,),
        in_specs=[pl.BlockSpec((rows, D), lambda i: (i, 0))] + [pl.BlockSpec(memory_space=pl.ANY)] * len(outs),
        out_specs=[pl.BlockSpec((None, rows, D), lambda i: (number, i, 0))],
        out_shape=[shape((2, FF, D), BF16)],
        input_output_aliases={1: 0} if outs else {},
        compiler_params=params(),
        cost_estimate=cost(1e8, 4 * D * FF),
        name="lay_out",
    )(gathered, *outs)


def moments(m, v, g):
    g = g.astype(F32)
    return 0.9 * m + 0.1 * g, 0.95 * v + 0.05 * g * g


def new_weight(w, m, v, g):
    m, v = moments(m, v, g)
    step = m * lax.rsqrt(v + 1e-8) + 0.1 * w.astype(F32)
    return (w.astype(F32) - 0.02 * step).astype(BF16)


class Line:
    def __init__(self):
        self.last = ()

    def run(self, f, first, *rest):
        first, self.last = lax.optimization_barrier((first, self.last))
        out = f(first, *rest)
        self.last = jax.tree.leaves(out)[-1:]
        return out


TILES = 4
PARTS = (3, 3, 2)
PARTS_OUT = ((4, 3, 3), (3, 4, 3))
UNITS = (2, 1, 1)
GROUPS = ((2, 1, 1), (2, 2))


def solution(mesh):
    def step(x, dy, w_gate, w_up, w_down, *state):
        m, v = state[:3], state[3:]
        x, dy = x[0], dy[0]
        place = lax.axis_index("dp").astype(jnp.int32).reshape(1)
        line = Line()
        queue, done, lays = [], {}, []
        outs = {"in": [], "out": []}
        groups = [(number, "out", (0, 1)) for number in (0, 1)]
        for number in (0, 1):
            first = 0
            for size in GROUPS[number]:
                groups.append((number, "in", tuple(range(first, first + size))))
                first += size

        def gather(number, kind, members):
            sums = [done[number, kind, one] for one in members]
            if kind == "in":
                first = members[0] * TILES
                new = line.run(update_in, place, sums, w_gate, w_up, m[:2], v[:2], number, first, TILES)
            else:
                new = line.run(update_out, place, sums, w_down, m[2], v[2], number)
            new = lax.all_gather(new, "dp", axis=0, tiled=True)

            def lay():
                if kind == "in":
                    outs["in"] = line.run(lay_in, new, outs["in"], number, first, TILES)
                else:
                    outs["out"] = line.run(lay_out, new, outs["out"], number)

            lays.append(lay)

        def run(room, f, *args):
            riding = queue[:room]
            del queue[:room]

            def beside(both, *rest):
                return f(both[0], *both[1], *rest)

            out, sums = line.run(beside, ([halves for _, halves in riding], args[:1]), *args[1:])
            for (name, _), one in zip(riding, sums):
                done[name] = one
            for group in list(groups):
                number, kind, members = group
                if all((number, kind, one) in done for one in members):
                    groups.remove(group)
                    gather(*group)
            return out

        def only(riders, _):
            return call(None, 1, [], [], (), riders, name="exchange")

        a0, at0 = line.run(prepare, x)
        act0, gate0, up0 = line.run(forward, a0, w_gate, w_up, 0)
        h1, a1, at1 = line.run(down, act0, x, w_down, 0)
        at0, at1 = (t.reshape(N, ROWS, T) for t in (at0, at1))

        so_far = []
        for k in range(N // TILES):
            so_far, halves = run(1, last_layer, a1, at1, dy, w_gate, w_up, w_down, 1, k * TILES, TILES, PARTS, so_far)
            queue.append(((1, "in", k), halves))
        dgate, dup, act1 = so_far
        for k, halves in enumerate(run(1, gradient_out, act1, dy, PARTS_OUT[1])):
            queue.append(((1, "out", k), halves))
        dh1 = run(1, states_backward, dgate, dup, w_gate, w_up, h1, dy, 1)
        for k, halves in enumerate(run(1, gradient_out, act0, dh1, PARTS_OUT[0])):
            queue.append(((0, "out", k), halves))
        k = 0
        for units in UNITS:
            for halves in run(2, first_layer, dh1, at0, gate0, up0, w_down, 0, k * TILES, units, PARTS):
                queue.append(((0, "in", k), halves))
                k += 1
        while queue:
            run(2, only, place)
        for lay in lays:
            lay()

        new_m, new_v = [], []
        for k in range(3):
            layers = []
            for number in range(2):
                if k == 2:
                    layers.append(jnp.concatenate([done[number, "out", q] for q in range(2)], axis=0))
                else:
                    columns = slice(k * TILES * TILE, (k + 1) * TILES * TILE)
                    layers.append(
                        jnp.concatenate([done[number, "in", q][:, columns] for q in range(N // TILES)], axis=1)
                    )
            one_m, one_v = moments(m[k], v[k], jnp.stack(layers))
            new_m.append(one_m)
            new_v.append(one_v)
        return (*outs["in"], *outs["out"], *new_m, *new_v)

    rows = P(None, "dp", None)
    return jax.shard_map(
        step,
        mesh=mesh,
        in_specs=(P(("rep", "dp")),) * 2 + (P(),) * 3 + (rows,) * 6,
        out_specs=(P("rep"),) * 3 + (P("rep", "dp", None),) * 6,
        check_vma=False,
    )
```

time: 2500 us -> 851 us (0.34)
  starting transfers between devices: 853 us -> 0.29 us
  Pallas kernels: 0 us -> 812 us
  matrix products: 657 us -> 0 us
  waiting for transfers between devices: 556 us -> 0.13 us
  other arithmetic: 285 us -> 10.3 us
  local copies, waits for them, and re-layouts: 121 us -> 5.81 us
    dot_general x102 -> x0, starting transfers between devices: 853 us -> none  [the longest x34 296 us: layer(): gate = jnp.dot(a, w['w_gate'], preferred_element_type=jnp.float32)]
    pallas_call x0 -> x28, Pallas kernels: none -> 812 us  [the longest x11 629 us: call(): pl.pallas_call(whole, grid=(steps,), in_specs=list(ins) + [pl.BlockSpec(m...]
    dot_general x57 -> x0, matrix products: 657 us -> none  [the longest x19 234 us: layer(): gate = jnp.dot(a, w['w_gate'], preferred_element_type=jnp.float32)]
    dot_general x102 -> x0, waiting for transfers between devices: 452 us -> none  [the longest x34 154 us: layer(): up = jnp.dot(a, w['w_up'], preferred_element_type=jnp.float32)]
    dot_general x96 -> x0, other arithmetic: 211 us -> none
    unnamed x66 -> x36, local copies, waits for them, and re-layouts: 117 us -> 5.63 us
    reshape x3 -> x0, waiting for transfers between devices: 104 us -> none  [step(): t.reshape(-1, *t.shape[2:])]
    convert_element_type x3 -> x0, other arithmetic: 33.2 us -> none  [the longest x1 27.5 us: layer(): (jax.nn.silu(gate) * up).astype(jnp.bfloat16)]
  transfers between devices with their start and end apart: 105 -> 7, of which waited for: 58 -> 0; matrix products, arithmetic and copies ran while one was open for 28% -> 1% of each run, Pallas kernels for 0% -> 67%
where the time goes in v1:
time: 851 us; the launch traced here: 844 us
  Pallas kernels  812 us (95%)
  between operations  15 us (2%)
  other arithmetic  10.3 us (1%)
    pallas_call x11, Pallas kernels, call(): pl.pallas_call(whole, grid=(steps,), in_specs=list(ins) + [pl.BlockSpec(m...  629 us
    pallas_call x1, Pallas kernels, forward(): pl.pallas_call(body, grid=(FF // TILE,), in_specs=[pl.BlockSpec((T, D), l...  52.2 us
    pallas_call x5, Pallas kernels, lay_in(): pl.pallas_call(body, grid=(D // rows, blocks), in_specs=[pl.BlockSpec((ro...  40.9 us
    pallas_call x1, Pallas kernels, down(): pl.pallas_call(body, grid=(T // rows,), in_specs=[pl.BlockSpec((rows, FF)...  31.4 us
    pallas_call x5, Pallas kernels, update_in(): pl.pallas_call(body, grid_spec=pltpu.PrefetchScalarGridSpec(num_scalar_pr...  22.5 us
    pallas_call x2, Pallas kernels, lay_out(): pl.pallas_call(body, grid=(FF // rows,), in_specs=[pl.BlockSpec((rows, D)...  20.3 us
  transfers between devices with their start and end apart: 7, of which 0 were waited for; matrix products, arithmetic and copies ran while one was open for 1% of the time, Pallas kernels for 67%

profile of v1, /device:TPU:0, one launch (start us, length us, event | category | flops | bytes accessed | tf_op | source)
XLA Modules:
  0.0 843.5 jit_solution(4522455103182029015)
XLA Ops:
  7.2 8.9 %prepare.1 = (bf16[2048,1280]{1,0:T(8,128)(2,1)}, bf16[1280,2048]{1,0:T(8,128)(2,1)}) custom-call(bf16[2048,1280]{1,0:T(8,128)(2,1)} %bitcast.30), custom_call_target="tpu_custom_call" | custom-call | flops 100000000 | bytes 16000000 | tf_op jit(solution)/shard_map/prepare/pallas_call | solution.py:220
  16.1 52.2 %forward.1 = (bf16[2048,4096]{1,0:T(8,128)(2,1)}, f32[2048,4096]{1,0:T(8,128)}, f32[2048,4096]{1,0:T(8,128)}) custom-call(bf16[2048,1280]{1,0:T(8,128)(2,1)} %get-tuple-element.221.a, bf16[2,1280,4096]{2,1,0:T(8,128)(2,1)} %refs_1_.3, bf16[2,1280,4096]{2,1,0:T(8,128)(2,1)} %refs_4_.17), custom_call_target="tpu_custom_call" | custom-call | flops 42949672960 | bytes 140000000 | tf_op jit(solution)/shard_map/forward/pallas_call | solution.py:199
  68.3 31.4 %down.1 = (bf16[2048,1280]{1,0:T(8,128)(2,1)}, bf16[2048,1280]{1,0:T(8,128)(2,1)}, bf16[1280,2048]{1,0:T(8,128)(2,1)}) custom-call(bf16[2048,4096]{1,0:T(8,128)(2,1)} %get-tuple-element.319.act.refs_0_, bf16[2048,1280]{1,0:T(8,128)(2,1)} %bitcast.31, bf16[2,4096,1280]{2,1,0:T(8,128)(2,1)} %refs_3_.23), custom_call_target="tpu_custom_call" | custom-call | flops 21474836480 | bytes 40000000 | tf_op jit(solution)/shard_map/down/pallas_call | solution.py:243
  99.7 42.0 %last_layer.4 = (bf16[2048,4096]{1,0:T(8,128)(2,1)}, bf16[2048,4096]{1,0:T(8,128)(2,1)}, bf16[2048,4096]{1,0:T(8,128)(2,1)}, bf16[8,80,768]{2,1,0:T(8,128)(2,1)}...) custom-call(bf16[2048,1280]{1,0:T(8,128)(2,1)} %get-tuple-element.26, ...), custom_call_target="tpu_custom_call" | custom-call | flops 26843545600 | bytes 32000000 | tf_op jit(solution)/shard_map/last_layer/pallas_call | solution.py:174
  141.8 51.7 %last_layer.5 = (bf16[2048,4096]{1,0:T(8,128)(2,1)}, bf16[2048,4096]{1,0:T(8,128)(2,1)}, bf16[2048,4096]{1,0:T(8,128)(2,1)}, bf16[8,80,768]{2,1,0:T(8,128)(2,1)}...) custom-call(bf16[2048,1280]{1,0:T(8,128)(2,1)} %get-tuple-element.26, ...), custom_call_target="tpu_custom_call", output_to_operand_aliasing={{0}: (6, {}), {1}: (7, {}), {2}: (8, {})} | custom-call | flops 26843545600 | bytes 32000000 | tf_op jit(solution)/shard_map/last_layer/pallas_call | solution.py:174
  193.4 48.8 %last_layer.6 = (bf16[2048,4096]{1,0:T(8,128)(2,1)}, bf16[2048,4096]{1,0:T(8,128)(2,1)}, bf16[2048,4096]{1,0:T(8,128)(2,1)}, bf16[8,80,768]{2,1,0:T(8,128)(2,1)}...) custom-call(bf16[2048,1280]{1,0:T(8,128)(2,1)} %get-tuple-element.26, ...), custom_call_target="tpu_custom_call", output_to_operand_aliasing={{0}: (6, {}), {1}: (7, {}), {2}: (8, {})} | custom-call | flops 26843545600 | bytes 32000000 | tf_op jit(solution)/shard_map/last_layer/pallas_call | solution.py:174
  242.2 4.8 update_in.5
  247.1 0.0 all-gather.18.cloned.1.call-start
  247.1 57.3 %last_layer.7 = (bf16[2048,4096]{1,0:T(8,128)(2,1)}, bf16[2048,4096]{1,0:T(8,128)(2,1)}, bf16[2048,4096]{1,0:T(8,128)(2,1)}, bf16[8,80,768]{2,1,0:T(8,128)(2,1)}...) custom-call(bf16[2048,1280]{1,0:T(8,128)(2,1)} %get-tuple-element.26, ...), custom_call_target="tpu_custom_call", output_to_operand_aliasing={{0}: (6, {}), {1}: (7, {}), {2}: (8, {})} | custom-call | flops 26843545600 | bytes 32000000 | tf_op jit(solution)/shard_map/last_layer/pallas_call | solution.py:174
  304.4 38.5 %gradient_out.2 = (bf16[8,128,384]{2,1,0:T(8,128)(2,1)}, bf16[8,128,512]{2,1,0:T(8,128)(2,1)}, bf16[8,128,384]{2,1,0:T(8,128)(2,1)}, bf16[8,128,384]{2,1,0:T(8,1...) custom-call(bf16[2048,4096]{1,0:T(8,128)(2,1)} %get-tuple-element.28, ...), custom_call_target="tpu_custom_call" | custom-call | flops 21474836480 | bytes 33000000 | tf_op jit(solution)/shard_map/gradient_out/pallas_call | solution.py:174
  342.9 4.8 update_in.6
  347.8 72.7 %states_backward.1 = (bf16[2048,1280]{1,0:T(8,128)(2,1)}, bf16[128,1280]{1,0:T(8,128)(2,1)}) custom-call(bf16[2048,4096]{1,0:T(8,128)(2,1)} %get-tuple-element.309.refs_0_, bf16[2048,4096]{1,0:T(8,128)(2,1)} %get-tuple-element.310.refs_1_, bf16[2,1280,4096]{2,1,0:T(8,128)(2,1)} %refs_1_.3, bf16[2,1280,4096]{2,1,0:T(8,128)(2,1)} %refs_4_.17, ...), custom_call_target="tpu_custom_call" | custom-call | flops 42949672960 | bytes 70000000 | tf_op jit(solution)/shard_map/states_backward/pallas_call | solution.py:174
  420.5 37.4 %gradient_out.3 = (bf16[8,128,512]{2,1,0:T(8,128)(2,1)}, bf16[8,128,384]{2,1,0:T(8,128)(2,1)}, bf16[8,128,384]{2,1,0:T(8,128)(2,1)}, bf16[8,128,512]{2,1,0:T(8,1...) custom-call(bf16[2048,4096]{1,0:T(8,128)(2,1)} %get-tuple-element.31, ...), custom_call_target="tpu_custom_call" | custom-call | flops 21474836480 | bytes 33000000 | tf_op jit(solution)/shard_map/gradient_out/pallas_call | solution.py:174
  458.0 3.3 update_out.2
  461.3 0.0 all-gather.14.cloned.1.call-start
  461.3 99.7 %first_layer.3 = (bf16[8,80,768]{2,1,0:T(8,128)(2,1)}, bf16[8,80,768]{2,1,0:T(8,128)(2,1)}, bf16[8,80,512]{2,1,0:T(8,128)(2,1)}, bf16[8,80,768]{2,1,0:T(8,128)(2...) custom-call(bf16[2048,1280]{1,0:T(8,128)(2,1)} %get-tuple-element.39, ...), custom_call_target="tpu_custom_call" | custom-call | flops 32212254720 | bytes 64000000 | tf_op jit(solution)/shard_map/first_layer/pallas_call | solution.py:174
  561.1 3.3 update_out.3
  564.4 0.0 all-gather.12.cloned.1.call-start
  564.4 87.8 %first_layer.4 = (bf16[8,80,768]{2,1,0:T(8,128)(2,1)}, bf16[8,80,768]{2,1,0:T(8,128)(2,1)}, bf16[8,80,512]{2,1,0:T(8,128)(2,1)}, bf16[8,80,768]{2,1,0:T(8,128)(2...) custom-call(bf16[2048,1280]{1,0:T(8,128)(2,1)} %get-tuple-element.39, ...), custom_call_target="tpu_custom_call" | custom-call | flops 16106127360 | bytes 32000000 | tf_op jit(solution)/shard_map/first_layer/pallas_call | solution.py:174
  652.2 4.8 update_in.7
  657.1 57.0 %first_layer.5 = (bf16[8,80,768]{2,1,0:T(8,128)(2,1)}, bf16[8,80,768]{2,1,0:T(8,128)(2,1)}, bf16[8,80,512]{2,1,0:T(8,128)(2,1)}, bf16[8,80,768]{2,1,0:T(8,128)(2...) custom-call(bf16[2048,1280]{1,0:T(8,128)(2,1)} %get-tuple-element.393.refs_1_.refs_0_, ...), custom_call_target="tpu_custom_call" | custom-call | flops 16106127360 | bytes 32000000 | tf_op jit(solution)/shard_map/first_layer/pallas_call | solution.py:174
  714.2 4.0 update_in.8
  718.2 0.0 all-gather.8.cloned.1.call-start
  718.2 36.3 %exchange.1.refs_0_ = bf16[80,2048]{1,0:T(8,128)(2,1)} custom-call(bf16[8,80,768]{2,1,0:T(8,128)(2,1)} %get-tuple-element.408.refs_0_, bf16[8,80,768]{2,1,0:T(8,128)(2,1)} %get-tuple-element.409.refs_1_, bf16[8,80,512]{2,1,0:T(8,128)(2,1)} %get-tuple-element.410.refs_2_, bf16[8,80,768]{2,1,0:T(8,128)(2,1)} %get-tuple-element.411.refs_3_, ...), custom_call_target="tpu_custom_call" | custom-call | tf_op jit(solution)/shard_map/exchange/pallas_call | solution.py:174
  754.6 4.1 update_in.9
  758.9 0.7 copy-done.13
  759.7 0.1 copy-done.6
  759.8 0.1 copy-done.7
  759.8 0.1 copy-done.8
  760.0 0.1 copy-done.14
  760.0 0.1 copy-done.15
  760.2 0.1 copy-done.16
  760.3 0.1 copy-done.17
  760.5 0.1 maximum_bitcast_fusion.1
  760.6 1.5 copy-done.4
  762.1 0.8 copy-done.5
  762.9 3.4 fusion.5
  766.4 1.0 copy-done.1
  767.4 3.5 fusion.3
  770.8 1.0 copy-done.3
  771.8 3.1 fusion.4
  774.9 10.1 %lay_in.5 = (bf16[2,1280,4096]{2,1,0:T(8,128)(2,1)}, bf16[2,1280,4096]{2,1,0:T(8,128)(2,1)}) custom-call(bf16[1280,4096]{1,0:T(8,128)(2,1)} %all-gather.20.cloned.1.call-done.gate.up, bf16[1280,4096]{1,0:T(8,128)(2,1)} %all-gather.20.cloned.1.call-done.gate.up), custom_call_target="tpu_custom_call" | custom-call | flops 100000000 | bytes 20000000 | tf_op jit(solution)/shard_map/lay_in/pallas_call | solution.py:557
  785.0 10.1 %lay_in.6 = (bf16[2,1280,4096]{2,1,0:T(8,128)(2,1)}, bf16[2,1280,4096]{2,1,0:T(8,128)(2,1)}) custom-call(bf16[1280,4096]{1,0:T(8,128)(2,1)} %all-gather.18.cloned.1.call-done.gate.up, bf16[1280,4096]{1,0:T(8,128)(2,1)} %all-gather.18.cloned.1.call-done.gate.up, ...), custom_call_target="tpu_custom_call", output_to_operand_aliasing={{0}: (2, {}), {1}: (3, {})} | custom-call | flops 100000000 | bytes 20000000 | tf_op jit(solution)/shard_map/lay_in/pallas_call | solution.py:557
  795.2 10.2 %lay_out.2.refs_0_ = bf16[2,4096,1280]{2,1,0:T(8,128)(2,1)} custom-call(bf16[4096,1280]{1,0:T(8,128)(2,1)} %all-gather.16.cloned.1.call-done.new), custom_call_target="tpu_custom_call" | custom-call | flops 100000000 | bytes 20971520 | tf_op jit(solution)/shard_map/lay_out/pallas_call | solution.py:580
  805.3 10.2 %lay_out.3 = bf16[2,4096,1280]{2,1,0:T(8,128)(2,1)} custom-call(bf16[4096,1280]{1,0:T(8,128)(2,1)} %all-gather.14.cloned.1.call-done.new, bf16[2,4096,1280]{2,1,0:T(8,128)(2,1)} %lay_out.2.refs_0_), custom_call_target="tpu_custom_call", output_to_operand_aliasing={{}: (1, {})} | custom-call | flops 100000000 | bytes 20971520 | tf_op jit(solution)/shard_map/lay_out/pallas_call | solution.py:580
  815.5 10.1 %lay_in.7 = (bf16[2,1280,4096]{2,1,0:T(8,128)(2,1)}, bf16[2,1280,4096]{2,1,0:T(8,128)(2,1)}) custom-call(bf16[1280,4096]{1,0:T(8,128)(2,1)} %all-gather.12.cloned.1.call-done.gate.up, bf16[1280,4096]{1,0:T(8,128)(2,1)} %all-gather.12.cloned.1.call-done.gate.up, ...), custom_call_target="tpu_custom_call", output_to_operand_aliasing={{0}: (2, {}), {1}: (3, {})} | custom-call | flops 100000000 | bytes 20000000 | tf_op jit(solution)/shard_map/lay_in/pallas_call | solution.py:557
  825.6 5.3 lay_in.8
  830.9 5.3 lay_in.9
  (52 shorter events, 0.7 us)
Async XLA Ops:
  7.2 767.8 %all-gather.20.cloned.1.call-start = ((), (), s32[]{:S(2)}) async-start(), calls=%async_computation.6 | async-start | bytes 11141120 | tf_op jit(solution)/shard_map/all_gather | solution.py:644
  247.1 538.0 %all-gather.18.cloned.1.call-start = ((), (), s32[]{:S(2)}) async-start(), calls=%async_computation.5 | async-start | bytes 11141120 | tf_op jit(solution)/shard_map/all_gather | solution.py:644
  347.7 447.4 %all-gather.16.cloned.1.call-start = ((), (), s32[]{:S(2)}) async-start(), calls=%async_computation.4 | async-start | bytes 11141120 | tf_op jit(solution)/shard_map/all_gather | solution.py:644
  461.3 344.0 %all-gather.14.cloned.1.call-start = ((), (), s32[]{:S(2)}) async-start(), calls=%async_computation.3 | async-start | bytes 11141120 | tf_op jit(solution)/shard_map/all_gather | solution.py:644
  564.4 251.1 %all-gather.12.cloned.1.call-start = ((), (), s32[]{:S(2)}) async-start(), calls=%async_computation.2 | async-start | bytes 11141120 | tf_op jit(solution)/shard_map/all_gather | solution.py:644
  657.0 168.5 %all-gather.10.cloned.1.call-start = ((), (), s32[]{:S(2)}) async-start(), calls=%async_computation.1 | async-start | bytes 5570560 | tf_op jit(solution)/shard_map/all_gather | solution.py:644
  718.2 112.7 %all-gather.8.cloned.1.call-start = ((), (), s32[]{:S(2)}) async-start(), calls=%async_computation | async-start | bytes 5570560 | tf_op jit(solution)/shard_map/all_gather | solution.py:644
  754.5 4.2 copy-start.9
  754.5 4.2 copy-start.10
  754.5 4.3 copy-start.12
  754.5 4.3 copy-start.11
  758.7 1.0 copy-start.13
  758.7 1.1 copy-start.6
  758.7 1.2 copy-start.7
  758.7 1.3 copy-start.8
  758.7 1.3 copy-start.14
  758.7 1.4 copy-start.15
  758.8 1.4 copy-start.16
  758.8 1.5 copy-start.17
  760.4 1.7 copy-start.4
  760.4 2.5 copy-start.5
  762.9 3.4 copy-start
  762.9 4.4 copy-start.1
  767.4 3.5 copy-start.2
  767.4 4.4 copy-start.3
Sparse Core Ops, SparseCore 0:
  247.2 67.0 all-gather.19
  347.9 71.2 all-gather.17
  461.4 79.7 all-gather.15
  564.5 81.8 all-gather.13
  657.2 68.2 all-gather.11
  727.6 42.4 all-gather.9
  772.3 38.3 all-gather.7

commit v2 on v1

--- a/solution.py
+++ b/solution.py
@@ -367,8 +367,9 @@
         outs, (rows, *held, loaded, put) = refs[: 6 * units], refs[6 * units :]
         begin, finish = gradients_in(at, rows, held, outs, (loaded, put), tiles, parts)
         begin()
-        _, dgate, dup = back(g[...], u[...], dot(dh[...], wd[...], 1, 1))
-        finish(dgate, dup)
+        some = [pl.ds(r * 512, 512) for r in range(T // 512)]
+        rows_of = [back(g[at, :], u[at, :], dot(dh[at, :], wd[...], 1, 1)) for at in some]
+        finish(jnp.concatenate([one[1] for one in rows_of]), jnp.concatenate([one[2] for one in rows_of]))
 
     full = pl.BlockSpec((T, D), lambda j: (0, 0), pipeline_mode=pl.Buffered(1))
     kept = pl.BlockSpec((T, TILE), lambda j: (0, first + j))
@@ -544,7 +545,7 @@
     )(place, *sums, w_down, m, v)
 
 
-def lay_in(gathered, outs, number, first, tiles):
+def lay_in(riders, gathered, outs, number, first, tiles):
     wide, rows = 512, 640
     each = tiles * TILE // wide
     blocks = gathered.shape[1] // 2 // wide
@@ -553,22 +554,24 @@
         refs[-2][...] = gate[...]
         refs[-1][...] = up[...]
 
-    out = pl.BlockSpec((None, rows, wide), lambda i, j: (number, i, first * TILE // wide + j))
-    return pl.pallas_call(
-        body,
-        grid=(D // rows, blocks),
-        in_specs=[
-            pl.BlockSpec((rows, wide), lambda i, j: (i, (j // each) * 2 * each + j % each)),
-            pl.BlockSpec((rows, wide), lambda i, j: (i, (j // each) * 2 * each + each + j % each)),
-        ]
+    def place(i, upper):
+        j = i // 2
+        return (i % 2, (j // each) * 2 * each + upper * each + j % each)
+
+    out = pl.BlockSpec((None, rows, wide), lambda i: (number, i % 2, first * TILE // wide + i // 2))
+    return call(
+        body,
+        2 * blocks,
+        [pl.BlockSpec((rows, wide), lambda i: place(i, 0)), pl.BlockSpec((rows, wide), lambda i: place(i, 1))]
         + [pl.BlockSpec(memory_space=pl.ANY)] * len(outs),
-        out_specs=[out, out],
-        out_shape=[shape((2, D, FF), BF16)] * 2,
-        input_output_aliases={2: 0, 3: 1} if outs else {},
-        compiler_params=params(),
-        cost_estimate=cost(1e8, 2e7),
+        [(out, shape((2, D, FF), BF16))] * 2,
+        (gathered, gathered, *outs),
+        riders,
+        aliases={2: 0, 3: 1} if outs else {},
+        flops=1e8,
+        nbytes=2e7,
         name="lay_in",
-    )(gathered, gathered, *outs)
+    )
 
 
 def lay_out(gathered, outs, number):
@@ -616,7 +619,7 @@
 PARTS = (3, 3, 2)
 PARTS_OUT = ((4, 3, 3), (3, 4, 3))
 UNITS = (2, 1, 1)
-GROUPS = ((2, 1, 1), (2, 2))
+GROUPS = ((2, 1, 1), (2, 1, 1))
 
 
 def solution(mesh):
@@ -634,6 +637,9 @@
                 groups.append((number, "in", tuple(range(first, first + size))))
                 first += size
 
+        def only(riders, _):
+            return call(None, 1, [], [], (), riders, name="exchange")
+
         def gather(number, kind, members):
             sums = [done[number, kind, one] for one in members]
             if kind == "in":
@@ -645,7 +651,7 @@
 
             def lay():
                 if kind == "in":
-                    outs["in"] = line.run(lay_in, new, outs["in"], number, first, TILES)
+                    outs["in"] = run(0, lay_in, new, outs["in"], number, first, TILES)
                 else:
                     outs["out"] = line.run(lay_out, new, outs["out"], number)
 
@@ -668,9 +674,6 @@
                     gather(*group)
             return out
 
-        def only(riders, _):
-            return call(None, 1, [], [], (), riders, name="exchange")
-
         a0, at0 = line.run(prepare, x)
         act0, gate0, up0 = line.run(forward, a0, w_gate, w_up, 0)
         h1, a1, at1 = line.run(down, act0, x, w_down, 0)
@@ -683,7 +686,7 @@
         dgate, dup, act1 = so_far
         for k, halves in enumerate(run(1, gradient_out, act1, dy, PARTS_OUT[1])):
             queue.append(((1, "out", k), halves))
-        dh1 = run(1, states_backward, dgate, dup, w_gate, w_up, h1, dy, 1)
+        dh1 = run(2, states_backward, dgate, dup, w_gate, w_up, h1, dy, 1)
         for k, halves in enumerate(run(1, gradient_out, act0, dh1, PARTS_OUT[0])):
             queue.append(((0, "out", k), halves))
         k = 0
@@ -693,8 +696,8 @@
                 k += 1
         while queue:
             run(2, only, place)
-        for lay in lays:
-            lay()
+        while lays:
+            lays.pop(0)()
 
         new_m, new_v = [], []
         for k in range(3):

time: 851 us -> 827 us (0.972)
  Pallas kernels: 812 us -> 788 us
    pallas_call x5 -> x0, Pallas kernels: 40.9 us -> none  [lay_in(): pl.pallas_call(body, grid=(D // rows, blocks), in_specs=[pl.BlockSpec((ro...]
    pallas_call x11 -> x17, Pallas kernels: 629 us -> 643 us  [call(): pl.pallas_call(whole, grid=(steps,), in_specs=list(ins) + [pl.BlockSpec(m...]
    pallas_call x5 -> x6, Pallas kernels: 22.5 us -> 25.7 us  [update_in(): pl.pallas_call(body, grid_spec=pltpu.PrefetchScalarGridSpec(num_scalar_pr...]
  transfers between devices with their start and end apart: 7 -> 8, of which waited for: 0 -> 0; matrix products, arithmetic and copies ran while one was open for 1% -> 1% of each run, Pallas kernels for 67% -> 66%
where the time goes in v2:
time: 827 us; the launch traced here: 819 us
  Pallas kernels  788 us (95%)
  between operations  14.6 us (2%)
  other arithmetic  10.3 us (1%)
    pallas_call x17, Pallas kernels, call(): pl.pallas_call(whole, grid=(steps,), in_specs=list(ins) + [pl.BlockSpec(m...  643 us
    pallas_call x1, Pallas kernels, forward(): pl.pallas_call(body, grid=(FF // TILE,), in_specs=[pl.BlockSpec((T, D), l...  52.2 us
    pallas_call x1, Pallas kernels, down(): pl.pallas_call(body, grid=(T // rows,), in_specs=[pl.BlockSpec((rows, FF)...  31.4 us
    pallas_call x6, Pallas kernels, update_in(): pl.pallas_call(body, grid_spec=pltpu.PrefetchScalarGridSpec(num_scalar_pr...  25.7 us
    pallas_call x2, Pallas kernels, lay_out(): pl.pallas_call(body, grid=(FF // rows,), in_specs=[pl.BlockSpec((rows, D)...  20.3 us
  transfers between devices with their start and end apart: 8, of which 0 were waited for; matrix products, arithmetic and copies ran while one was open for 1% of the time, Pallas kernels for 66%

profile of v2, /device:TPU:0, one launch (start us, length us, event | category | flops | bytes accessed | tf_op | source)
XLA Modules:
  0.0 819.3 jit_solution(13320008694834392855)
XLA Ops:
  7.2 8.9 %prepare.1 = (bf16[2048,1280]{1,0:T(8,128)(2,1)}, bf16[1280,2048]{1,0:T(8,128)(2,1)}) custom-call(bf16[2048,1280]{1,0:T(8,128)(2,1)} %bitcast.30), custom_call_target="tpu_custom_call" | custom-call | flops 100000000 | bytes 16000000 | tf_op jit(solution)/shard_map/prepare/pallas_call | solution.py:220
  16.1 52.2 %forward.1 = (bf16[2048,4096]{1,0:T(8,128)(2,1)}, f32[2048,4096]{1,0:T(8,128)}, f32[2048,4096]{1,0:T(8,128)}) custom-call(bf16[2048,1280]{1,0:T(8,128)(2,1)} %get-tuple-element.225.a, bf16[2,1280,4096]{2,1,0:T(8,128)(2,1)} %refs_1_.7, bf16[2,1280,4096]{2,1,0:T(8,128)(2,1)} %refs_4_.19), custom_call_target="tpu_custom_call" | custom-call | flops 42949672960 | bytes 140000000 | tf_op jit(solution)/shard_map/forward/pallas_call | solution.py:199
  68.3 31.4 %down.1 = (bf16[2048,1280]{1,0:T(8,128)(2,1)}, bf16[2048,1280]{1,0:T(8,128)(2,1)}, bf16[1280,2048]{1,0:T(8,128)(2,1)}) custom-call(bf16[2048,4096]{1,0:T(8,128)(2,1)} %get-tuple-element.332.act.refs_0_, bf16[2048,1280]{1,0:T(8,128)(2,1)} %bitcast.31, bf16[2,4096,1280]{2,1,0:T(8,128)(2,1)} %refs_3_.25), custom_call_target="tpu_custom_call" | custom-call | flops 21474836480 | bytes 40000000 | tf_op jit(solution)/shard_map/down/pallas_call | solution.py:243
  99.7 42.2 %last_layer.4 = (bf16[2048,4096]{1,0:T(8,128)(2,1)}, bf16[2048,4096]{1,0:T(8,128)(2,1)}, bf16[2048,4096]{1,0:T(8,128)(2,1)}, bf16[8,80,768]{2,1,0:T(8,128)(2,1)}...) custom-call(bf16[2048,1280]{1,0:T(8,128)(2,1)} %get-tuple-element.27, ...), custom_call_target="tpu_custom_call" | custom-call | flops 26843545600 | bytes 32000000 | tf_op jit(solution)/shard_map/last_layer/pallas_call | solution.py:174
  142.0 51.3 %last_layer.5 = (bf16[2048,4096]{1,0:T(8,128)(2,1)}, bf16[2048,4096]{1,0:T(8,128)(2,1)}, bf16[2048,4096]{1,0:T(8,128)(2,1)}, bf16[8,80,768]{2,1,0:T(8,128)(2,1)}...) custom-call(bf16[2048,1280]{1,0:T(8,128)(2,1)} %get-tuple-element.27, ...), custom_call_target="tpu_custom_call", output_to_operand_aliasing={{0}: (6, {}), {1}: (7, {}), {2}: (8, {})} | custom-call | flops 26843545600 | bytes 32000000 | tf_op jit(solution)/shard_map/last_layer/pallas_call | solution.py:174
  193.3 49.0 %last_layer.6 = (bf16[2048,4096]{1,0:T(8,128)(2,1)}, bf16[2048,4096]{1,0:T(8,128)(2,1)}, bf16[2048,4096]{1,0:T(8,128)(2,1)}, bf16[8,80,768]{2,1,0:T(8,128)(2,1)}...) custom-call(bf16[2048,1280]{1,0:T(8,128)(2,1)} %get-tuple-element.27, ...), custom_call_target="tpu_custom_call", output_to_operand_aliasing={{0}: (6, {}), {1}: (7, {}), {2}: (8, {})} | custom-call | flops 26843545600 | bytes 32000000 | tf_op jit(solution)/shard_map/last_layer/pallas_call | solution.py:174
  242.3 4.8 update_in.6
  247.1 57.7 %last_layer.7 = (bf16[2048,4096]{1,0:T(8,128)(2,1)}, bf16[2048,4096]{1,0:T(8,128)(2,1)}, bf16[2048,4096]{1,0:T(8,128)(2,1)}, bf16[8,80,768]{2,1,0:T(8,128)(2,1)}...) custom-call(bf16[2048,1280]{1,0:T(8,128)(2,1)} %get-tuple-element.27, ...), custom_call_target="tpu_custom_call", output_to_operand_aliasing={{0}: (6, {}), {1}: (7, {}), {2}: (8, {})} | custom-call | flops 26843545600 | bytes 32000000 | tf_op jit(solution)/shard_map/last_layer/pallas_call | solution.py:174
  304.8 4.0 update_in.7
  308.9 43.6 %gradient_out.2 = (bf16[8,128,384]{2,1,0:T(8,128)(2,1)}, bf16[8,128,512]{2,1,0:T(8,128)(2,1)}, bf16[8,128,384]{2,1,0:T(8,128)(2,1)}, bf16[8,128,384]{2,1,0:T(8,1...) custom-call(bf16[2048,4096]{1,0:T(8,128)(2,1)} %get-tuple-element.29, ...), custom_call_target="tpu_custom_call" | custom-call | flops 21474836480 | bytes 33000000 | tf_op jit(solution)/shard_map/gradient_out/pallas_call | solution.py:174
  352.5 4.0 update_in.8
  356.5 0.0 all-gather.17.cloned.1.call-start
  356.6 89.1 %states_backward.1 = (bf16[2048,1280]{1,0:T(8,128)(2,1)}, bf16[128,1280]{1,0:T(8,128)(2,1)}, bf16[128,1280]{1,0:T(8,128)(2,1)}) custom-call(bf16[2048,4096]{1,0:T(8,128)(2,1)} %get-tuple-element.314.refs_0_, bf16[2048,4096]{1,0:T(8,128)(2,1)} %get-tuple-element.315.refs_1_, bf16[2,1280,4096]{2,1,0:T(8,128)(2,1)} %refs_1_.7, bf16[2,1280,4096]{2,1,0:T(8,128)(2,1)} %refs_4_.19, ...), custom_call_target="tpu_custom_call" | custom-call | flops 42949672960 | bytes 70000000 | tf_op jit(solution)/shard_map/states_backward/pallas_call | solution.py:174
  445.7 3.3 update_out.2
  449.0 0.0 all-gather.15.cloned.1.call-start
  449.0 32.7 %gradient_out.3 = (bf16[8,128,512]{2,1,0:T(8,128)(2,1)}, bf16[8,128,384]{2,1,0:T(8,128)(2,1)}, bf16[8,128,384]{2,1,0:T(8,128)(2,1)}, bf16[8,128,512]{2,1,0:T(8,1...) custom-call(bf16[2048,4096]{1,0:T(8,128)(2,1)} %get-tuple-element.33, ...), custom_call_target="tpu_custom_call" | custom-call | flops 21474836480 | bytes 33000000 | tf_op jit(solution)/shard_map/gradient_out/pallas_call | solution.py:174
  481.7 70.2 %first_layer.3 = (bf16[8,80,768]{2,1,0:T(8,128)(2,1)}, bf16[8,80,768]{2,1,0:T(8,128)(2,1)}, bf16[8,80,512]{2,1,0:T(8,128)(2,1)}, bf16[8,80,768]{2,1,0:T(8,128)(2...) custom-call(bf16[2048,1280]{1,0:T(8,128)(2,1)} %get-tuple-element.39, ...), custom_call_target="tpu_custom_call" | custom-call | flops 32212254720 | bytes 64000000 | tf_op jit(solution)/shard_map/first_layer/pallas_call | solution.py:174
  552.0 3.3 update_out.3
  555.3 81.1 %first_layer.4 = (bf16[8,80,768]{2,1,0:T(8,128)(2,1)}, bf16[8,80,768]{2,1,0:T(8,128)(2,1)}, bf16[8,80,512]{2,1,0:T(8,128)(2,1)}, bf16[8,80,768]{2,1,0:T(8,128)(2...) custom-call(bf16[2048,1280]{1,0:T(8,128)(2,1)} %get-tuple-element.39, ...), custom_call_target="tpu_custom_call" | custom-call | flops 16106127360 | bytes 32000000 | tf_op jit(solution)/shard_map/first_layer/pallas_call | solution.py:174
  636.5 4.8 update_in.9
  641.3 50.0 %first_layer.5 = (bf16[8,80,768]{2,1,0:T(8,128)(2,1)}, bf16[8,80,768]{2,1,0:T(8,128)(2,1)}, bf16[8,80,512]{2,1,0:T(8,128)(2,1)}, bf16[8,80,768]{2,1,0:T(8,128)(2...) custom-call(bf16[2048,1280]{1,0:T(8,128)(2,1)} %get-tuple-element.398.refs_1_.refs_0_, ...), custom_call_target="tpu_custom_call" | custom-call | flops 16106127360 | bytes 32000000 | tf_op jit(solution)/shard_map/first_layer/pallas_call | solution.py:174
  691.4 4.0 update_in.10
  695.5 34.6 %exchange.1.refs_0_ = bf16[80,2048]{1,0:T(8,128)(2,1)} custom-call(bf16[8,80,768]{2,1,0:T(8,128)(2,1)} %get-tuple-element.413.refs_0_, bf16[8,80,768]{2,1,0:T(8,128)(2,1)} %get-tuple-element.414.refs_1_, bf16[8,80,512]{2,1,0:T(8,128)(2,1)} %get-tuple-element.415.refs_2_, bf16[8,80,768]{2,1,0:T(8,128)(2,1)} %get-tuple-element.416.refs_3_, ...), custom_call_target="tpu_custom_call" | custom-call | tf_op jit(solution)/shard_map/exchange/pallas_call | solution.py:174
  730.1 4.1 update_in.11
  734.5 0.7 copy-done.13
  735.2 0.1 copy-done.6
  735.3 0.1 copy-done.7
  735.4 0.1 copy-done.8
  735.5 0.1 copy-done.14
  735.6 0.1 copy-done.15
  735.7 0.1 copy-done.16
  735.8 0.1 copy-done.17
  736.1 0.1 maximum_bitcast_fusion.1
  736.2 1.5 copy-done.4
  737.7 0.8 copy-done.5
  738.5 3.4 fusion.5
  741.9 1.0 copy-done.1
  742.9 3.5 fusion.3
  746.4 1.0 copy-done.3
  747.3 3.1 fusion.4
  750.5 10.1 %lay_in.6 = (bf16[2,1280,4096]{2,1,0:T(8,128)(2,1)}, bf16[2,1280,4096]{2,1,0:T(8,128)(2,1)}) custom-call(bf16[1280,4096]{1,0:T(8,128)(2,1)} %all-gather.23.cloned.1.call-done.refs_0_.refs_1_, bf16[1280,4096]{1,0:T(8,128)(2,1)} %all-gather.23.cloned.1.call-done.refs_0_.refs_1_), custom_call_target="tpu_custom_call" | custom-call | flops 100000000 | bytes 20000000 | tf_op jit(solution)/shard_map/lay_in/pallas_call | solution.py:174
  760.6 5.3 lay_in.7
  765.9 5.3 lay_in.8
  771.2 10.2 %lay_out.2.refs_0_ = bf16[2,4096,1280]{2,1,0:T(8,128)(2,1)} custom-call(bf16[4096,1280]{1,0:T(8,128)(2,1)} %all-gather.17.cloned.1.call-done.new), custom_call_target="tpu_custom_call" | custom-call | flops 100000000 | bytes 20971520 | tf_op jit(solution)/shard_map/lay_out/pallas_call | solution.py:583
  781.4 10.2 %lay_out.3 = bf16[2,4096,1280]{2,1,0:T(8,128)(2,1)} custom-call(bf16[4096,1280]{1,0:T(8,128)(2,1)} %all-gather.15.cloned.1.call-done.new, bf16[2,4096,1280]{2,1,0:T(8,128)(2,1)} %lay_out.2.refs_0_), custom_call_target="tpu_custom_call", output_to_operand_aliasing={{}: (1, {})} | custom-call | flops 100000000 | bytes 20971520 | tf_op jit(solution)/shard_map/lay_out/pallas_call | solution.py:583
  791.5 10.1 %lay_in.9 = (bf16[2,1280,4096]{2,1,0:T(8,128)(2,1)}, bf16[2,1280,4096]{2,1,0:T(8,128)(2,1)}) custom-call(bf16[1280,4096]{1,0:T(8,128)(2,1)} %all-gather.13.cloned.1.call-done.refs_0_.refs_1_, bf16[1280,4096]{1,0:T(8,128)(2,1)} %all-gather.13.cloned.1.call-done.refs_0_.refs_1_, ...), custom_call_target="tpu_custom_call", output_to_operand_aliasing={{0}: (2, {}), {1}: (3, {})} | custom-call | flops 100000000 | bytes 20000000 | tf_op jit(solution)/shard_map/lay_in/pallas_call | solution.py:174
  801.6 5.3 lay_in.10
  806.9 5.3 lay_in.11
  (57 shorter events, 0.8 us)
Async XLA Ops:
  7.2 743.3 %all-gather.23.cloned.1.call-start = ((), (), s32[]{:S(2)}) async-start(), calls=%async_computation.7 | async-start | bytes 11141120 | tf_op jit(solution)/shard_map/all_gather | solution.py:650
  247.1 513.5 %all-gather.21.cloned.1.call-start = ((), (), s32[]{:S(2)}) async-start(), calls=%async_computation.6 | async-start | bytes 5570560 | tf_op jit(solution)/shard_map/all_gather | solution.py:650
  308.9 457.0 %all-gather.19.cloned.1.call-start = ((), (), s32[]{:S(2)}) async-start(), calls=%async_computation.5 | async-start | bytes 5570560 | tf_op jit(solution)/shard_map/all_gather | solution.py:650
  356.5 414.7 %all-gather.17.cloned.1.call-start = ((), (), s32[]{:S(2)}) async-start(), calls=%async_computation.4 | async-start | bytes 11141120 | tf_op jit(solution)/shard_map/all_gather | solution.py:650
  449.0 332.4 %all-gather.15.cloned.1.call-start = ((), (), s32[]{:S(2)}) async-start(), calls=%async_computation.3 | async-start | bytes 11141120 | tf_op jit(solution)/shard_map/all_gather | solution.py:650
  555.3 236.2 %all-gather.13.cloned.1.call-start = ((), (), s32[]{:S(2)}) async-start(), calls=%async_computation.2 | async-start | bytes 11141120 | tf_op jit(solution)/shard_map/all_gather | solution.py:650
  641.3 160.3 %all-gather.11.cloned.1.call-start = ((), (), s32[]{:S(2)}) async-start(), calls=%async_computation.1 | async-start | bytes 5570560 | tf_op jit(solution)/shard_map/all_gather | solution.py:650
  695.4 111.5 %all-gather.9.cloned.1.call-start = ((), (), s32[]{:S(2)}) async-start(), calls=%async_computation | async-start | bytes 5570560 | tf_op jit(solution)/shard_map/all_gather | solution.py:650
  730.1 4.2 copy-start.9
  730.1 4.2 copy-start.10
  730.1 4.3 copy-start.11
  730.1 4.3 copy-start.12
  734.2 1.0 copy-start.13
  734.2 1.1 copy-start.6
  734.2 1.2 copy-start.7
  734.2 1.3 copy-start.8
  734.3 1.3 copy-start.14
  734.3 1.4 copy-start.15
  734.4 1.4 copy-start.16
  734.4 1.5 copy-start.17
  735.9 1.7 copy-start.4
  736.0 2.5 copy-start.5
  738.5 3.4 copy-start
  738.5 4.4 copy-start.1
  742.9 3.5 copy-start.2
  742.9 4.4 copy-start.3
Sparse Core Ops, SparseCore 0:
  247.2 66.3 all-gather.22
  315.9 46.0 all-gather.20
  364.2 52.7 all-gather.18
  449.1 58.2 all-gather.16
  555.4 81.5 all-gather.14
  641.4 64.0 all-gather.12
  707.8 42.0 all-gather.10
  752.1 38.3 all-gather.8
